TPU v7x, 128 devices: a whole 4x4x4 slice. The times are simulated.
128 devices in a mesh: row: 8 (over z, y_hi), col: 16 (over y_lo, x, core).
Axes of the slice: x: 4, y: 4 (y_hi: 2, y_lo: 2; y = y_hi * 2 + y_lo), z: 4, core: 2. Of those that a mesh axis runs over, the one named last changes fastest.
Arguments:
- matrix: float32 [16, 1024, 8, 2048], P(None, 'row', None, 'col'), may hold values from -150 to 150
- inverse_rest: float32 [16, 1024, 7, 2048], P(None, 'row', None, 'col'), may hold values from -6 to 6
- upper_block: float32 [2, 1024, 1, 2048], P(None, 'row', None, 'col'), may hold values from -6 to 6, as said below
- lower_below: float32 [2, 1024, 7, 2048], P(None, 'row', None, 'col'), may hold values from -0.046875 to 0.046875
- lower_inverse: float32 [2, 1024, 2048], P(None, 'row', 'col'), may hold values from -1 to 1, as said below
Outputs:
- plus_rows: float32 [2, 1024, 8, 2048], P(None, 'row', None, 'col')
Inputs may be any that keep to these rules, and one draw needn't show every extreme that they name: `upper_block`: upper triangular. `lower_inverse`: unit lower triangular.
All inputs are finite; a program needn't handle non-finite values.
Results may differ from a plain program's by a relative error of at most 0.000052.
Values sent between devices are 32-bit elements; how exact they have to be, the bound alone decides.
A program may use at most 192 MiB of HBM per device.

v0:
```python
import jax
import jax.numpy as jnp
from jax import lax
from jax.sharding import Mesh
from jax.sharding import PartitionSpec as P

ROW = ("row_0", "row_1")
COL = ("col_0", "col_1", "col_2")
ROW_COL = ("row_0", "row_1", "col_0", "col_1", "col_2")


def over_axes(array, axes):
    for axis in axes:
        array = lax.psum(array, axis)
    return array


def laid_out(pieces, dim):
    lengths = list(pieces.shape[1:])
    lengths[dim] *= pieces.shape[0]
    return jnp.moveaxis(pieces, 0, dim).reshape(lengths)


def from_everyone(array, axis):
    count = lax.axis_size(axis)
    return lax.all_to_all(
        jnp.broadcast_to(array[None], (count, *array.shape)), axis, 0, 0, tiled=True
    )


def collect(array, axis, dim):
    return laid_out(from_everyone(array, axis), dim)


def dot_exact(left, right, form):
    return jnp.einsum(
        form, left, right, precision=lax.Precision.HIGHEST, preferred_element_type=jnp.float32
    )


def mirror(panel_rows, row_devices, col_devices, panel_cycles, blk_size):
    share_rows, col_ratio, width_all = panel_rows.shape
    sectioned = panel_rows.reshape(share_rows, col_ratio, 1, panel_cycles, row_devices, blk_size)
    sectioned = lax.all_to_all(sectioned, ROW, split_axis=4, concat_axis=2, tiled=True)
    sectioned = sectioned.reshape(share_rows, col_devices, panel_cycles, blk_size)
    sectioned = lax.all_to_all(sectioned, COL, split_axis=1, concat_axis=0, tiled=True)
    return sectioned.reshape(col_devices * share_rows, panel_cycles * blk_size)


def per_device(matrix, inverse_rest, upper_block, lower_below, lower_inverse):
    row_devices = lax.axis_size(ROW)
    col_devices = lax.axis_size(COL)
    col_ratio = col_devices // row_devices
    row_cycles, blk_size, col_cycles, blk_again = matrix.shape
    panel_cycles = lower_inverse.shape[0]
    width_all = lower_inverse.shape[2] * col_devices
    rest_local = inverse_rest.shape[2] * blk_size
    panel_col_cycles = upper_block.shape[2]
    local_rows = col_cycles * blk_size
    share_rows = local_rows // col_devices
    matrix_sq = jnp.sum(matrix * matrix)
    rest_sq = jnp.sum(inverse_rest * inverse_rest)
    matrix_total, rest_total = (over_axes(matrix_sq, ROW_COL), over_axes(rest_sq, ROW_COL))
    below_all = lax.all_gather(lower_below, ROW, axis=1, tiled=True).reshape(width_all, rest_local)
    inverse_rows = (
        inverse_rest.reshape(col_cycles, col_ratio, blk_size, rest_local)
        .transpose(0, 2, 1, 3)
        .reshape(local_rows, col_ratio, rest_local)
    )
    padded = jnp.concatenate(
        [
            upper_block,
            jnp.zeros(
                (row_cycles - panel_cycles, blk_size, panel_col_cycles, blk_size), jnp.float32
            ),
        ],
        axis=0,
    )
    upper_rows = (
        padded.reshape(col_cycles, col_ratio, blk_size, panel_col_cycles * blk_size)
        .transpose(0, 2, 1, 3)
        .reshape(local_rows, col_ratio, panel_col_cycles, 1, blk_size)
    )
    owner_mask = lax.broadcasted_iota(jnp.int32, (1, 1, 1, col_devices, 1), 3) == lax.axis_index(
        COL
    )
    spread = jnp.where(owner_mask, upper_rows, 0.0).reshape(
        share_rows * lax.axis_size(COL), col_ratio, width_all
    )
    panel_share = lax.psum_scatter(
        spread - dot_exact(inverse_rows, below_all, "usm,tm->ust"),
        COL,
        scatter_dimension=0,
        tiled=True,
    )
    factor_rows = collect(lower_inverse, ROW, 1)
    factor_all = lax.all_gather(factor_rows, COL, axis=2, tiled=True).reshape(width_all, width_all)
    inverse_share = dot_exact(panel_share, factor_all, "ust,tw->usw")
    panel_sq = jnp.sum(inverse_share * inverse_share)
    mirrored = mirror(inverse_share, row_devices, col_devices, panel_cycles, blk_size)
    inverse_block = mirrored.reshape(col_cycles, blk_size, panel_cycles, blk_size).transpose(
        2, 3, 0, 1
    )
    panel_total = over_axes(panel_sq, ROW_COL)
    balance = jnp.sqrt(jnp.sqrt((rest_total + panel_total) / matrix_total))
    return 0.5 * (balance * matrix[:panel_cycles] + inverse_block / balance)


def solution(mesh):
    split = Mesh(mesh.devices.reshape(4, 2, 2, 4, 2), ("row_0", "row_1", "col_0", "col_1", "col_2"))
    return jax.shard_map(
        per_device,
        mesh=split,
        in_specs=(
            P(None, ROW, None, COL),
            P(None, ROW, None, COL),
            P(None, ROW, None, COL),
            P(None, ROW, None, COL),
            P(None, ROW, COL),
        ),
        out_specs=P(None, ROW, None, COL),
        check_vma=False,
    )
```

profile of v0, /device:TPU:1, one launch (start us, length us, event | category | flops | bytes accessed | tf_op | source)
XLA Modules:
  0.0 415.5 jit_solution(5951134886269617252)
XLA Ops:
  6.5 0.7 all-gather.3.cloned.1.call-update
  7.3 1.0 broadcast_in_dim.42
  8.3 27.6 %all_to_all.29 = f32[8,2,128,128]{3,2,1,0:T(8,128)S(1)} all-to-all(f32[8,2,128,128]{3,2,1,0:T(8,128)S(1)} %broadcast_in_dim.42), channel_id=1, replica_groups=mesh['row_0'=4,'row_1'=2,'col_0'=2,'col_1'=4,'col_2'=2] {'row_0','row_1'}, dimensions={0} | all-to-all | bytes 2097152 | tf_op jit(solution)/shard_map/all_to_all | solution.py:26
  35.9 1.1 copy.41
  37.0 1.0 concatenate.3
  38.2 6.8 %broadcast_in_dim.39 = f32[1024,2,16,128]{3,2,0,1:T(8,128)} broadcast(f32[1024,2,128]{2,0,1:T(8,128)S(1)} %bitcast.51), dimensions={0,1,3} | broadcast | bytes 17825792 | tf_op jit(solution)/shard_map/jit(_where)/broadcast_in_dim | solution.py:87
  45.0 18.1 %broadcast_in_dim.40 = f32[1024,2,2048]{2,0,1:T(8,128)} reshape(f32[1024,2,16,128]{3,2,0,1:T(8,128)} %broadcast_in_dim.39) | data formatting | bytes 33554432 | tf_op jit(solution)/shard_map/jit(_where)/broadcast_in_dim | solution.py:87
  63.1 8.6 %copy.37 = f32[16,128,7,128]{1,3,2,0:T(8,128)} copy(f32[16,128,7,128]{3,1,2,0:T(8,128)} %param.6) | data formatting | bytes 14680064 | tf_op args[1]
  71.7 8.1 %copy.38 = f32[8,128,2,896]{3,1,0,2:T(8,128)} copy(f32[8,128,2,896]{1,3,2,0:T(8,128)} %bitcast.48) | data formatting | bytes 14680064 | tf_op jit(solution)/shard_map/transpose | solution.py:67
  79.9 33.9 %all-gather.3.cloned.1.call-done = f32[2,1024,7,128]{3,1,2,0:T(8,128)} async-done(((f32[2,128,7,128]{3,1,2,0:T(8,128)}), f32[2,1024,7,128]{3,1,2,0:T(8,128)}) %all-gather.3.cloned.1.call-update) | async-done | bytes 7340048 | tf_op jit(solution)/shard_map/all_gather | solution.py:64
  113.8 11.8 %copy.39 = f32[2,1024,7,128]{1,0,3,2:T(2,128)} copy(f32[2,1024,7,128]{3,1,2,0:T(8,128)} %all-gather.3.cloned.1.call-done) | data formatting | bytes 14680064 | tf_op jit(solution)/shard_map/all_gather | solution.py:64
  125.6 10.7 %reshape.58 = f32[2048,896,1]{0,1,2:T(8,128)} reshape(f32[2,1024,7,128]{1,0,3,2:T(2,128)} %copy.39) | data formatting | bytes 14680064 | tf_op jit(solution)/shard_map/reshape | solution.py:64
  136.3 60.3 %select_subtract_fusion = f32[1024,2,2048]{2,0,1:T(8,128)} fusion(f32[1024,2,2048]{2,0,1:T(8,128)} %broadcast_in_dim.40, pred[2048]{0:T(1024)(128)(4,1)S(1)} %broadcast_bitcast_fusion, f32[1024,2,896]{2,0,1:T(8,128)} %bitcast.49, f32[2048,896,1]{0,1,2:T(8,128)} %reshape.58), kind=kOutput, calls=%fused_computation | convolution fusion | flops 45105545216 | bytes 48236544 | tf_op jit(solution)/shard_map/usm,tm->ust/dot_general | solution.py:36
  196.6 15.5 %all-gather.5.cloned.1.call-done = f32[2,1024,2048]{2,1,0:T(8,128)} async-done(((f32[2,1024,128]{2,1,0:T(8,128)}), f32[2,1024,2048]{2,1,0:T(8,128)}) %all-gather.5.cloned.1.call-update) | async-done | bytes 16777232 | tf_op jit(solution)/shard_map/all_gather | solution.py:97
  212.1 98.9 %reduce-scatter.2.cloned.1.call-done = f32[64,2,2048]{2,0,1:T(8,128)} async-done(((f32[1024,2,2048]{2,0,1:T(8,128)}), f32[64,2,2048]{2,0,1:T(8,128)}) %reduce-scatter.2.cloned.1.call-update) | async-done | bytes 1048592 | tf_op jit(solution)/shard_map/reduce_scatter | solution.py:90
  310.9 13.6 %multiply_reduce_fusion.2 = (f32[]{:T(128)}, f32[64,2,2048]{2,0,1:T(8,128)S(1)}) fusion(f32[64,2,2048]{2,0,1:T(8,128)} %reduce-scatter.2.cloned.1.call-done, f32[2048,2048,1]{1,0,2:T(8,128)} %bitcast.47), kind=kOutput, calls=%fused_computation.6 | convolution fusion | flops 6442975232 | bytes 18874372 | tf_op jit(solution)/shard_map/ust,tw->usw/dot_general | solution.py:36
  324.5 0.2 copy.51
  324.7 0.8 copy.43
  325.5 21.3 %all_to_all.30 = f32[64,2,1,2,8,128]{5,1,3,0,2,4:T(2,128)S(1)} all-to-all(f32[64,2,1,2,8,128]{5,1,3,0,2,4:T(2,128)S(1)} %copy.43), channel_id=1, replica_groups=mesh['row_0'=4,'row_1'=2,'col_0'=2,'col_1'=4,'col_2'=2] {'row_0','row_1'}, dimensions={4} | all-to-all | bytes 2097152 | tf_op jit(solution)/shard_map/all_to_all | solution.py:44
  346.8 0.6 copy.54
  347.5 1.5 copy.45
  349.0 7.3 %all-to-all-start.2 = ((f32[64,16,2,128]{3,2,0,1:T(2,128)}), f32[64,16,2,128]{3,2,0,1:T(2,128)S(1)}, u32[]{:S(2)}, u32[]{:S(2)}) async-start(f32[64,16,2,128]{3,2,0,1:T(2,128)} %copy.45), calls=%async_computation.3 | async-start | bytes 2097152 | tf_op jit(solution)/shard_map/all_to_all | solution.py:46
  356.3 5.7 %multiply_reduce_fusion.1 = f32[]{:T(128)} fusion(f32[16,128,7,128]{3,1,2,0:T(8,128)} %param.6), kind=kLoop, calls=%fused_computation.2 | loop fusion | flops 3670015 | bytes 7340036 | tf_op jit(solution)/shard_map/reduce_sum | solution.py:62
  361.9 6.2 %multiply_reduce_fusion = f32[]{:T(128)} fusion(f32[16,128,8,128]{3,2,1,0:T(8,128)} %param.5), kind=kLoop, calls=%fused_computation.1 | loop fusion | flops 4194303 | bytes 8388612 | tf_op jit(solution)/shard_map/reduce_sum | solution.py:61
  369.3 0.4 copy.50
  369.7 7.1 %all-reduce.2 = (f32[]{:T(128)}, f32[]{:T(128)}) all-reduce(f32[]{:T(128)S(6)} %add.48, f32[]{:T(128)} %multiply_reduce_fusion), channel_id=1, replica_groups=mesh['row_0'=4,'row_1'=2,'col_0'=2,'col_1'=4,'col_2'=2] {'row_0'}, use_global_device_ids=true, to_apply=%region_1.0 | all-reduce | flops 2 | bytes 16 | tf_op jit(solution)/shard_map/psum | solution.py:14
  376.7 5.9 %all-reduce.5 = (f32[]{:T(128)}, f32[]{:T(128)}) all-reduce(f32[]{:T(128)} %get-tuple-element.7, f32[]{:T(128)} %get-tuple-element.8), channel_id=1, replica_groups=mesh['row_0'=4,'row_1'=2,'col_0'=2,'col_1'=4,'col_2'=2] {'row_1'}, use_global_device_ids=true, to_apply=%region_2.0 | all-reduce | flops 2 | bytes 16 | tf_op jit(solution)/shard_map/psum | solution.py:14
  382.7 4.5 %all-reduce.4 = (f32[]{:T(128)}, f32[]{:T(128)}) all-reduce(f32[]{:T(128)} %get-tuple-element.13, f32[]{:T(128)} %get-tuple-element.14), channel_id=1, replica_groups=mesh['row_0'=4,'row_1'=2,'col_0'=2,'col_1'=4,'col_2'=2] {'col_0'}, use_global_device_ids=true, to_apply=%region_3.0 | all-reduce | flops 2 | bytes 16 | tf_op jit(solution)/shard_map/psum | solution.py:14
  387.1 9.2 %all-reduce.1 = (f32[]{:T(128)}, f32[]{:T(128)}) all-reduce(f32[]{:T(128)} %get-tuple-element.11, f32[]{:T(128)} %get-tuple-element.12), channel_id=1, replica_groups=mesh['row_0'=4,'row_1'=2,'col_0'=2,'col_1'=4,'col_2'=2] {'col_1'}, use_global_device_ids=true, to_apply=%region_4.0 | all-reduce | flops 2 | bytes 16 | tf_op jit(solution)/shard_map/psum | solution.py:14
  396.3 9.6 %all-reduce.3 = (f32[]{:T(128)}, f32[]{:T(128)}) all-reduce(f32[]{:T(128)} %get-tuple-element.5, f32[]{:T(128)} %get-tuple-element.6), channel_id=1, replica_groups=mesh['row_0'=4,'row_1'=2,'col_0'=2,'col_1'=4,'col_2'=2] {'col_2'}, use_global_device_ids=true, to_apply=%region_5.0 | all-reduce | flops 2 | bytes 16 | tf_op jit(solution)/shard_map/psum | solution.py:14
  407.5 0.1 add_multiply_fusion
  407.6 1.3 copy.47
  (12 shorter events, 0.4 us)
Async XLA Ops:
  6.5 107.3 %all-gather.3.cloned.1.call-start = ((), (), s32[]{:S(2)}) async-start(), calls=%async_computation.4 | async-start | bytes 8257536 | tf_op jit(solution)/shard_map/all_gather | solution.py:64
  7.3 204.8 %all-gather.5.cloned.1.call-start = ((), (), s32[]{:S(2)}) async-start(), calls=%async_computation.6 | async-start | bytes 17825792 | tf_op jit(solution)/shard_map/all_gather | solution.py:97
  37.0 273.9 %reduce-scatter.2.cloned.1.call-start = ((), (), s32[]{:S(2)}) async-start(), calls=%async_computation.5 | async-start | bytes 17825792 | tf_op jit(solution)/shard_map/reduce_scatter | solution.py:90
  349.0 58.4 %all-to-all-start.2 = ((f32[64,16,2,128]{3,2,0,1:T(2,128)}), f32[64,16,2,128]{3,2,0,1:T(2,128)S(1)}, u32[]{:S(2)}, u32[]{:S(2)}) async-start(f32[64,16,2,128]{3,2,0,1:T(2,128)} %copy.45), calls=%async_computation.3 | async-start | bytes 2097152 | tf_op jit(solution)/shard_map/all_to_all | solution.py:46
  356.3 13.0 %slice-start = ((f32[16,128,8,128]{3,2,1,0:T(8,128)}), f32[2,128,8,128]{3,2,1,0:T(8,128)S(1)}, s32[]{:S(2)}) async-start(f32[16,128,8,128]{3,2,1,0:T(8,128)} %param.5), calls=%async_computation.7 | async-start | bytes 2097152 | tf_op jit(solution)/shard_map/slice | solution.py:106
Sparse Core Ops, SparseCore 0:
  9.6 104.1 all-gather.2
  115.4 96.6 all-gather.4
  214.5 96.4 reduce-scatter.1
where the time goes:
time: 417 us; the launch traced here: 415 us
  waiting for transfers between devices  149 us (36%)
  blocking collectives  85.1 us (20%)
  matrix products  73.9 us (18%)
  local copies, waits for them, and re-layouts  72.2 us (17%)
  between operations  15.8 us (4%)
  other arithmetic  12.2 us (3%)
  starting transfers between devices  7.39 us (2%)
    reduce_scatter x1, waiting for transfers between devices, per_device(): lax.psum_scatter(spread - dot_exact(inverse_rows, below_all, 'usm,tm->ust...  98.9 us
    dot_general x2, matrix products, dot_exact(): jnp.einsum(form, left, right, precision=lax.Precision.HIGHEST, preferred_...  73.9 us
    psum x5, blocking collectives, over_axes(): array = lax.psum(array, axis)  36.2 us
    all_gather x1, waiting for transfers between devices, per_device(): lax.all_gather(lower_below, ROW, axis=1, tiled=True)  33.9 us
    all_to_all x1, blocking collectives, from_everyone(): lax.all_to_all(jnp.broadcast_to(array[None], (count, *array.shape)), axis...  27.6 us
    broadcast_in_dim x3, local copies, waits for them, and re-layouts, per_device(): jnp.where(owner_mask, upper_rows, 0.0)  25 us
    all_to_all x1, blocking collectives, mirror(): lax.all_to_all(sectioned, ROW, split_axis=4, concat_axis=2, tiled=True)  21.3 us
    all_gather x1, waiting for transfers between devices, per_device(): lax.all_gather(factor_rows, COL, axis=2, tiled=True)  15.5 us
  transfers between devices with their start and end apart: 4, of which 3 were waited for; matrix products, arithmetic and copies ran while one was open for 34% of the time, Pallas kernels for 0%

commit v1 on v0

v1 whole, which is shorter than its diff:
```python
import jax
import jax.numpy as jnp
from jax import lax
from jax.experimental import pallas as pl
from jax.experimental.pallas import tpu as pltpu
from jax.sharding import Mesh
from jax.sharding import PartitionSpec as P

ROW = ("row_0", "row_1")
COL = ("col_0", "col_1", "col_2")
MESH = pl.DeviceIdType.MESH
F32 = jnp.float32
BF16 = jnp.bfloat16
ANY = pl.ANY

S_BELOW = 0
S_FWD = 16
S_PAIR = 18
S_A = 26
S_B = 42
S_Y = 58
S_L = 66
S_OUT = 77
S_M1 = 78
S_M2 = 86
S_SUM = 94
N_SEM = 104


def split(value):
    hi = value.astype(BF16)
    lo = (value - hi.astype(F32)).astype(BF16)
    return hi, lo


def dot_t(a, b):
    return lax.dot_general(a, b, (((1,), (1,)), ((), ())), preferred_element_type=F32)


def dot_n(a, b):
    return lax.dot_general(a, b, (((1,), (0,)), ((), ())), preferred_element_type=F32)


def rows_at(block, count):
    return pl.ds(pl.multiple_of(block * 128, 128), count * 128)


def kernel(
    mat, rest, up, below, linv, out,
    ball, yfwd, rcat, bcat, part, pair, rec_a, rec_b, rec_y, xy, xs, lall, acc, acc_in,
    m1, m2, top, mstage, rstage, ublk, lstage, sums, sums_in,
    in_sem, r_sem, m_sem, send, recv,
):
    z = lax.axis_index("row_0")
    yh = lax.axis_index("row_1")
    yl = lax.axis_index("col_0")
    x = lax.axis_index("col_1")
    h = lax.axis_index("col_2")
    me_r = z * 2 + yh

    def dev(dz=0, dyh=0, dyl=0, dx=0, dh=0):
        return ((z + dz) % 4, (yh + dyh) % 2, (yl + dyl) % 2, (x + dx) % 4, (h + dh) % 2)

    y = yh * 2 + yl

    def dev_y(dy):
        there = (y + dy) % 4
        return (z, there // 2, there % 2, x, h)

    def copy(src, dst, index, device):
        return pltpu.make_async_remote_copy(
            src_ref=src, dst_ref=dst, send_sem=send.at[index], recv_sem=recv.at[index],
            device_id=device, device_id_type=MESH,
        )

    partner = dev(dh=1)
    zp, zm = dev(dz=1), dev(dz=3)
    xp, xm = dev(dx=1), dev(dx=3)
    yp, ym = dev_y(1), dev_y(3)
    ypair = dev(dyl=1)

    load_below = [pltpu.make_async_copy(below.at[k], ball.at[me_r, k], in_sem.at[k]) for k in range(2)]
    load_l = pltpu.make_async_copy(linv, lstage, in_sem.at[2])
    load_u = pltpu.make_async_copy(up, ublk, in_sem.at[3])
    load_top = pltpu.make_async_copy(mat.at[pl.ds(0, 2)], top, in_sem.at[4])
    for load in (*load_below, load_l, load_u):
        load.start()

    def load_r(p):
        return pltpu.make_async_copy(rest.at[p], rstage.at[p % 2], r_sem.at[p % 2])

    def load_m(p):
        return pltpu.make_async_copy(mat.at[p], mstage.at[p % 2], m_sem.at[p % 2])

    load_r(0).start()
    load_r(1).start()
    load_top.start()

    barrier = pltpu.get_barrier_semaphore()
    friends = [dev(dz=dz, dyh=dyh) for dz in range(4) for dyh in range(2) if (dz, dyh) != (0, 0)]
    friends += [dev(dx=dx, dh=dh) for dx in range(4) for dh in range(2) if (dx, dh) != (0, 0)]
    friends += [yp, ym]
    for friend in friends:
        pl.semaphore_signal(barrier, inc=1, device_id=friend, device_id_type=MESH)
    pl.semaphore_wait(barrier, len(friends))

    def below_copy(source, half, step, device):
        ref = ball.at[source, half]
        return copy(ref, ref, S_BELOW + 2 * step + half, device)

    for load in load_below:
        load.wait()
    below_copy(me_r, 0, 1, zp).start()
    below_copy(me_r, 1, 2, zm).start()
    copy(ball.at[me_r, 0], yfwd.at[0], S_FWD, yp).start()
    copy(ball.at[me_r, 1], yfwd.at[1], S_FWD + 1, ym).start()
    below_copy(me_r, 1, 1, zp).start()
    below_copy(me_r, 0, 2, zm).start()

    my_pair = lall.at[yl, yh, z, x]
    load_l.wait()
    swap_l = copy(lstage.at[1 - h], lall.at[yl, yh, z, x, :, pl.ds(pl.multiple_of(h * 128, 128), 128)], S_L, partner)
    swap_l.start()
    for core in range(2):
        @pl.when(h == core)
        def _():
            lall[yl, yh, z, x, :, core * 128:(core + 1) * 128] = lstage[core]

    mine_l = jnp.logical_or(h == 1, yl == 0)
    beside_l = jnp.logical_or(h == 1, yl == 1)

    def spread_l(ref, base, which):
        for j in range(1, 4):
            yield copy(ref, ref, base + j - 1, dev(dx=j) if which == "x" else dev(dz=j))

    def l_copy(index, dy):
        ref = lall.at[yl, yh]
        return copy(ref, ref, S_L + index, dev_y(dy))

    def l_forward(index, from_dy, to_dy, first):
        there = (y + from_dy) % 4
        ref = lall.at[there % 2, there // 2, pl.ds(first, 2)]
        return copy(ref, ref, S_L + index, dev_y(to_dy))

    sums[...] = jnp.zeros(sums.shape, F32)

    def take_r(p, carry):
        load_r(p).wait()
        base = ((p // 4) * 4 + (p % 2) * 2 + (p // 2) % 2) * 128
        total = jnp.zeros((8, 128), F32)
        for q in range(7):
            value = rstage[p % 2, q]
            total += jnp.sum((value * value).reshape(16, 8, 128), axis=0)
            hi, lo = split(value)
            where = pl.ds(pl.multiple_of(base, 128), 128)
            rcat[where, q * 128:(q + 1) * 128] = hi
            rcat[where, (7 + q) * 128:(8 + q) * 128] = lo
        sums[0, 1] += total

        @pl.when(p + 2 < 16)
        def _():
            load_r(p + 2).start()

        return carry

    lax.fori_loop(0, 16, take_r, 0)
    load_u.wait()

    def source(step):
        j = step % 4
        dz = jnp.where(j == 1, 3, jnp.where(j == 2, 1, jnp.where(j == 3, 2, 0)))
        return (z + dz) % 4, (yh + step // 4) % 2

    def pair_copy(s):
        return copy(part.at[s % 4, 1 - h], pair.at[s], S_PAIR + s, partner)

    def a_copy(s, side):
        far = (x + 2) % 4
        src = part.at[s % 4, h, rows_at(far * 4 + 2 * side, 2)]
        return copy(src, rec_a.at[s, side], S_A + 2 * s + side, xp if side == 0 else xm)

    def b_copy(s, side):
        near = (x + (1 if side == 0 else 3)) % 4
        src = part.at[s % 4, h, rows_at(near * 4, 4)]
        return copy(src, rec_b.at[s, side], S_B + 2 * s + side, xp if side == 0 else xm)

    def y_copy(s):
        return copy(xy.at[s, rows_at((1 - yl) * 2, 2)], rec_y.at[s], S_Y + s, ypair)

    def step_body(t, carry):
        @pl.when(t < 8)
        def _():
            load_m(2 * t).start()
            load_m(2 * t + 1).start()

        @pl.when(jnp.logical_and(t >= 1, t < 9))
        def _():
            s = t - 1
            pair_copy(s).wait_recv()

            def add(i, carry):
                where = rows_at(((i + 4 * (x + 2)) % 16), 1)
                part[s % 4, h, where] += pair[s, where]
                return carry

            lax.fori_loop(0, 4, add, 0)
            a_copy(s, 0).start()
            a_copy(s, 1).start()
            lax.fori_loop(4, 16, add, 0)

        @pl.when(jnp.logical_and(t >= 2, t < 10))
        def _():
            s = t - 2
            for side in range(2):
                a_copy(s, side).wait_recv()
                near = (x + (1 if side == 0 else 3)) % 4
                where = rows_at(near * 4 + 2 * side, 2)
                part[s % 4, h, where] += rec_a[s, side]
                b_copy(s, side).start()

        @pl.when(t == 1)
        def _():
            below_copy(source(1)[0] * 2 + source(1)[1], 0, 1, zp).wait_recv()
            below_copy(source(1)[0] * 2 + source(1)[1], 0, 3, zp).start()
            below_copy(source(2)[0] * 2 + source(2)[1], 1, 2, zm).wait_recv()
            below_copy(source(2)[0] * 2 + source(2)[1], 1, 3, zm).start()
            copy(yfwd.at[0], yfwd.at[0], S_FWD, yp).wait_recv()
            copy(yfwd.at[1], yfwd.at[1], S_FWD + 1, ym).wait_recv()
            back = (y + 3) % 4
            copy(yfwd.at[0], ball.at[z * 2 + back // 2, 0], S_BELOW + 8, yp).start()
            ahead = (y + 1) % 4
            copy(yfwd.at[1], ball.at[z * 2 + ahead // 2, 1], S_BELOW + 9, ym).start()
            swap_l.wait_recv()

            @pl.when(mine_l)
            def _():
                for c in spread_l(my_pair, S_L + 1, "x"):
                    c.start()

        @pl.when(t == 2)
        def _():
            r4 = source(4)[0] * 2 + source(4)[1]
            below_copy(r4, 0, 4, zp).wait_recv()
            below_copy(r4, 1, 4, zp).wait_recv()
            below_copy(r4, 0, 5, zp).start()
            below_copy(r4, 1, 6, zm).start()
            below_copy(r4, 1, 5, zp).start()
            below_copy(r4, 0, 6, zm).start()

            @pl.when(mine_l)
            def _():
                for c in spread_l(my_pair, S_L + 1, "x"):
                    c.wait_recv()
                for c in spread_l(lall.at[yl, yh, z], S_L + 4, "z"):
                    c.start()

        @pl.when(t == 3)
        def _():
            @pl.when(mine_l)
            def _():
                for c in spread_l(lall.at[yl, yh, z], S_L + 4, "z"):
                    c.wait_recv()
                l_copy(7, 1).start()
                l_copy(8, 3).start()

        @pl.when(t == 5)
        def _():
            r5 = source(5)[0] * 2 + source(5)[1]
            below_copy(r5, 0, 5, zp).wait_recv()
            below_copy(r5, 0, 7, zp).start()
            r6 = source(6)[0] * 2 + source(6)[1]
            below_copy(r6, 1, 6, zm).wait_recv()
            below_copy(r6, 1, 7, zm).start()

        @pl.when(t == 8)
        def _():
            @pl.when(beside_l)
            def _():
                l_copy(7, 1).wait_recv()
                l_forward(9, 3, 1, 0).start()
                l_copy(8, 3).wait_recv()
                l_forward(10, 1, 3, 2).start()

        @pl.when(t < 8)
        def _():
            zs, ys = source(t)
            r = zs * 2 + ys
            seen0 = jnp.logical_or(jnp.logical_or(t == 0, t == 1), jnp.logical_or(t == 4, t == 5))
            seen1 = jnp.logical_or(jnp.logical_or(t == 0, t == 2), jnp.logical_or(t == 4, t == 6))

            @pl.when(jnp.logical_not(seen0))
            def _():
                below_copy(r, 0, t, zp).wait_recv()

            @pl.when(jnp.logical_not(seen1))
            def _():
                below_copy(r, 1, t, zp).wait_recv()

            for k in range(2):
                for q in range(7):
                    hi, lo = split(ball[r, k, q])
                    where = slice(k * 128, (k + 1) * 128)
                    bcat[where, q * 128:(q + 1) * 128] = hi
                    bcat[where, (7 + q) * 128:(8 + q) * 128] = hi
                    bcat[where, (14 + q) * 128:(15 + q) * 128] = lo

            def tile(i, carry):
                where = rows_at(2 * i, 2)
                value = dot_t(rcat[where, 0:1792], bcat[:, 0:1792]) + dot_t(rcat[where, 0:896], bcat[:, 1792:2688])
                part[t % 4, 0, where] = value[:, :128]
                part[t % 4, 1, where] = value[:, 128:]
                return carry

            lax.fori_loop(0, 8, tile, 0)

            @pl.when((yl * 8 + x * 2 + h) % 8 == r)
            def _():
                for k in range(2):
                    part[t % 4, yl, k * 256:k * 256 + 128] -= ublk[k]

            pair_copy(t).start()

            for slot in range(2):
                load_m(2 * t + slot).wait()
                value = mstage[slot]
                sums[0, 0] += jnp.sum((value * value).reshape(128, 8, 128), axis=0)

        @pl.when(jnp.logical_and(t >= 3, t < 11))
        def _():
            s = t - 3
            b_copy(s, 0).wait_recv()
            b_copy(s, 1).wait_recv()

            def add(i, carry):
                where = rows_at(i, 1)
                xy[s, where] = part[s % 4, h, rows_at(x * 4 + i, 1)] + rec_b[s, 0, where] + rec_b[s, 1, where]
                return carry

            lax.fori_loop(0, 4, add, 0)
            y_copy(s).start()
            pair_copy(s).wait_send()
            for side in range(2):
                a_copy(s, side).wait_send()
                b_copy(s, side).wait_send()

        @pl.when(t >= 4)
        def _():
            s = t - 4
            y_copy(s).wait_recv()
            value = xy[s, rows_at(yl * 2, 2)] + rec_y[s]
            hi, lo = split(value)
            xs[s, :, 0:128] = hi
            xs[s, :, 128:256] = lo

        return carry

    lax.fori_loop(0, 12, step_body, 0)

    @pl.when(mine_l)
    def _():
        l_forward(9, 3, 1, 0).wait_recv()
        l_forward(10, 1, 3, 2).wait_recv()

    n_pairs = 4 + 4 * h

    def clear(i, carry):
        acc[i] = jnp.zeros((256, 256), F32)
        return carry

    lax.fori_loop(0, n_pairs, clear, 0)

    def product(s, carry):
        zs, ys = source(s)

        def one(i, carry):
            hi, lo = split(lall[i // 4, ys, zs, i % 4])
            acc[i] += dot_n(xs[s], jnp.concatenate([hi, hi], axis=0)) + dot_n(xs[s, :, 0:128], lo)
            return carry

        lax.fori_loop(0, n_pairs, one, 0)
        return carry

    lax.fori_loop(0, 8, product, 0)

    out_copy = copy(acc.at[pl.ds(0, 4)], acc_in, S_OUT, partner)

    @pl.when(h == 1)
    def _():
        out_copy.start()

    @pl.when(h == 0)
    def _():
        out_copy.wait_recv()

        def add(i, carry):
            acc[i] += acc_in[i]
            return carry

        lax.fori_loop(0, 4, add, 0)

    def squares(i, carry):
        value = acc[4 * h + i]
        value = value * value
        sums[0, 1] += jnp.sum((value[:, :128] + value[:, 128:]).reshape(32, 8, 128), axis=0)
        return carry

    lax.fori_loop(0, 4, squares, 0)

    def sum_copy(phase, slot, device):
        return copy(sums.at[phase], sums_in.at[3 * phase + slot], S_SUM + 3 * phase + slot - (2 if phase else 0), device)

    def sum_copies(phase):
        if phase == 0:
            return [sum_copy(0, 0, partner)]
        make = (None, lambda j: dev(dx=j), dev_y, lambda j: dev(dz=j))[phase]
        return [sum_copy(phase, j - 1, make(j)) for j in range(1, 4)]

    for c in sum_copies(0):
        c.start()

    def mirror_row(j):
        dz, dy = j // 2, j % 2
        to_z, to_y = (z + dz) % 4, (yh + dy) % 2
        src = acc.at[4 * h + to_z, :, pl.ds(pl.multiple_of(to_y * 128, 128), 128)]
        return copy(src, m1.at[me_r], S_M1 + j, dev(dz=dz, dyh=dy))

    def mirror_row_in(j):
        from_z, from_y = (z + 4 - j // 2) % 4, (yh + j % 2) % 2
        ref = m1.at[from_z * 2 + from_y]
        return copy(ref, ref, S_M1 + j, zp)

    for j in range(1, 8):
        mirror_row(j).start()
    for side in range(2):
        @pl.when(yh == side)
        def _():
            m1[me_r] = acc[4 * h + z, :, side * 128:(side + 1) * 128]

    for phase in range(4):
        copies = sum_copies(phase)
        for c in copies:
            c.wait_recv()
        total = sums[phase]
        for slot in range(len(copies)):
            total += sums_in[3 * phase + slot]
        sums[phase + 1] = total
        if phase < 3:
            for c in sum_copies(phase + 1):
                c.start()

    def mirror_col(j):
        dx, dh = j // 2, j % 2
        to_x, to_h = (x + dx) % 4, (h + dh) % 2
        return copy(m1.at[to_x * 2 + to_h], m2.at[h, x], S_M2 + j, dev(dx=dx, dh=dh))

    def mirror_col_in(j):
        from_x, from_h = (x + 4 - j // 2) % 4, (h + j % 2) % 2
        ref = m2.at[from_h, from_x]
        return copy(ref, ref, S_M2 + j, xp)

    for j in range(1, 8):
        mirror_row_in(j).wait_recv()
    for j in range(1, 8):
        mirror_col(j).start()
    m2[h, x] = m1[x * 2 + h]

    load_top.wait()
    total = sums[4]
    ratio = jnp.sum(total[1], axis=(0, 1), keepdims=True) / jnp.sum(total[0], axis=(0, 1), keepdims=True)
    balance = jnp.sqrt(jnp.sqrt(ratio))
    half = 0.5 * balance
    inverse = -0.5 / balance
    for j in range(1, 8):
        mirror_col_in(j).wait_recv()
    for k in range(2):
        for m in range(8):
            block = m2[k, m // 2, (m % 2) * 128:(m % 2 + 1) * 128]
            where = pl.ds(m, 128, stride=8)
            out[k, where, :] = half * top[k, where, :] + inverse * block.T

    for step in range(1, 8):
        for side in range(2):
            below_copy(me_r, side, step, zp).wait_send()
    for side in range(2):
        copy(ball.at[me_r, side], yfwd.at[side], S_FWD + side, yp).wait_send()
    swap_l.wait_send()

    @pl.when(mine_l)
    def _():
        for c in spread_l(my_pair, S_L + 1, "x"):
            c.wait_send()
        for c in spread_l(lall.at[yl, yh, z], S_L + 4, "z"):
            c.wait_send()
        l_copy(7, 1).wait_send()
        l_copy(8, 3).wait_send()

    @pl.when(beside_l)
    def _():
        l_forward(9, 3, 1, 0).wait_send()
        l_forward(10, 1, 3, 2).wait_send()

    def last_y(s, carry):
        y_copy(s).wait_send()
        return carry

    lax.fori_loop(0, 8, last_y, 0)

    @pl.when(h == 1)
    def _():
        out_copy.wait_send()

    for j in range(1, 8):
        mirror_row(j).wait_send()
        mirror_col(j).wait_send()
    for phase in range(4):
        for c in sum_copies(phase):
            c.wait_send()


def per_device(matrix, inverse_rest, upper_block, lower_below, lower_inverse):
    vmem = pltpu.VMEM
    dma = pltpu.SemaphoreType.DMA
    result = pl.pallas_call(
        kernel,
        out_shape=jax.ShapeDtypeStruct((2, 1024, 128), F32),
        in_specs=[pl.BlockSpec(memory_space=ANY)] * 5,
        out_specs=pl.BlockSpec(memory_space=pltpu.VMEM),
        scratch_shapes=[
            vmem((8, 2, 7, 128, 128), F32),
            vmem((2, 7, 128, 128), F32),
            vmem((2048, 1792), BF16),
            vmem((256, 2688), BF16),
            vmem((4, 2, 2048, 128), F32),
            vmem((8, 2048, 128), F32),
            vmem((8, 2, 256, 128), F32),
            vmem((8, 2, 512, 128), F32),
            vmem((8, 256, 128), F32),
            vmem((8, 512, 128), F32),
            vmem((8, 256, 256), BF16),
            vmem((2, 2, 4, 4, 128, 256), F32),
            vmem((8, 256, 256), F32),
            vmem((4, 256, 256), F32),
            vmem((8, 256, 128), F32),
            vmem((2, 4, 256, 128), F32),
            vmem((2, 1024, 128), F32),
            vmem((2, 1024, 128), F32),
            vmem((2, 7, 128, 128), F32),
            vmem((2, 128, 128), F32),
            vmem((2, 128, 128), F32),
            vmem((5, 2, 8, 128), F32),
            vmem((12, 2, 8, 128), F32),
            dma((5,)),
            dma((2,)),
            dma((2,)),
            dma((N_SEM,)),
            dma((N_SEM,)),
        ],
        compiler_params=pltpu.CompilerParams(
            collective_id=0, has_side_effects=True, vmem_limit_bytes=67043328
        ),
    )(
        matrix.reshape(16, 1024, 128),
        inverse_rest.transpose(0, 2, 1, 3),
        upper_block.reshape(2, 128, 128),
        lower_below.transpose(0, 2, 1, 3),
        lower_inverse,
    )
    return result.reshape(2, 128, 8, 128)


def solution(mesh):
    split_mesh = Mesh(mesh.devices.reshape(4, 2, 2, 4, 2), ("row_0", "row_1", "col_0", "col_1", "col_2"))
    return jax.shard_map(
        per_device,
        mesh=split_mesh,
        in_specs=(
            P(None, ROW, None, COL),
            P(None, ROW, None, COL),
            P(None, ROW, None, COL),
            P(None, ROW, None, COL),
            P(None, ROW, COL),
        ),
        out_specs=P(None, ROW, None, COL),
        check_vma=False,
    )
```

time: 417 us -> 238 us (0.57)
  Pallas kernels: 0 us -> 235 us
  waiting for transfers between devices: 149 us -> 0 us
  blocking collectives: 85.1 us -> 0 us
  matrix products: 73.9 us -> 0 us
  local copies, waits for them, and re-layouts: 72.2 us -> 2.26 us
  between operations: 15.8 us -> 0.01 us
  other arithmetic: 12.2 us -> 0 us
  starting transfers between devices: 7.39 us -> 0 us
    pallas_call x0 -> x1, Pallas kernels: none -> 235 us  [per_device(): pl.pallas_call(kernel, out_shape=jax.ShapeDtypeStruct((2, 1024, 128), F32...]
    reduce_scatter x1 -> x0, waiting for transfers between devices: 98.9 us -> none  [per_device(): lax.psum_scatter(spread - dot_exact(inverse_rows, below_all, 'usm,tm->ust...]
    dot_general x2 -> x0, matrix products: 73.9 us -> none  [dot_exact(): jnp.einsum(form, left, right, precision=lax.Precision.HIGHEST, preferred_...]
    all_gather x2 -> x0, waiting for transfers between devices: 49.4 us -> none  [the longest x1 33.9 us: per_device(): lax.all_gather(lower_below, ROW, axis=1, tiled=True)]
    all_to_all x2 -> x0, blocking collectives: 48.9 us -> none  [the longest x1 27.6 us: from_everyone(): lax.all_to_all(jnp.broadcast_to(array[None], (count, *array.shape)), axis...]
    psum x5 -> x0, blocking collectives: 36.2 us -> none  [over_axes(): array = lax.psum(array, axis)]
    broadcast_in_dim x4 -> x0, local copies, waits for them, and re-layouts: 26 us -> none  [the longest x3 25 us: per_device(): jnp.where(owner_mask, upper_rows, 0.0)]
    reshape x3 -> x0, local copies, waits for them, and re-layouts: 13 us -> none  [the longest x1 10.7 us: per_device(): lax.all_gather(lower_below, ROW, axis=1, tiled=True)]
  transfers between devices with their start and end apart: 4 -> 0, of which waited for: 3 -> 0; matrix products, arithmetic and copies ran while one was open for 34% -> 0% of each run, Pallas kernels for 0% -> 0%
where the time goes in v1:
time: 238 us; the launch traced here: 237 us
  Pallas kernels  235 us (99%)
    pallas_call x1, Pallas kernels, per_device(): pl.pallas_call(kernel, out_shape=jax.ShapeDtypeStruct((2, 1024, 128), F32...  235 us

profile of v1, /device:TPU:1, one launch (start us, length us, event | category | flops | bytes accessed | tf_op | source)
XLA Modules:
  0.0 237.4 jit_solution(11397900314686002401)
XLA Ops:
  0.0 235.1 %shard_map.55 = f32[2,1024,128]{2,1,0:T(8,128)} custom-call(f32[16,1024,128]{2,1,0:T(8,128)} %bitcast.5, f32[16,7,128,128]{3,2,1,0:T(8,128)} %bitcast.6, f32[2,128,128]{2,1,0:T(8,128)} %bitcast.9, f32[2,7,128,128]{3,2,1,0:T(8,128)} %bitcast.8, f32[2,128,128]{2,1,0:T(8,128)} %linv.1), custom_call_target="tpu_custom_call" | custom-call | tf_op jit(solution)/shard_map/pallas_call | solution.py:523
  235.2 2.3 copy.7

commit v2 on v1

v2 whole, which is shorter than its diff:
```python
import jax
import jax.numpy as jnp
from jax import lax
from jax.experimental import pallas as pl
from jax.experimental.pallas import tpu as pltpu
from jax.sharding import Mesh
from jax.sharding import PartitionSpec as P

ROW = ("row_0", "row_1")
COL = ("col_0", "col_1", "col_2")
MESH = pl.DeviceIdType.MESH
F32 = jnp.float32
BF16 = jnp.bfloat16
ANY = pl.ANY

S_BELOW = 0
S_FWD = 16
S_PAIR = 18
S_A = 50
S_B = 66
S_Y = 82
S_L = 90
S_LY = 98
S_OUT = 146
S_M1 = 150
S_M2 = 158
S_SUM = 166
N_SEM = 176


def split(value):
    hi = value.astype(BF16)
    lo = (value - hi.astype(F32)).astype(BF16)
    return hi, lo


def dot_t(a, b):
    return lax.dot_general(a, b, (((1,), (1,)), ((), ())), preferred_element_type=F32)


def dot_n(a, b):
    return lax.dot_general(a, b, (((1,), (0,)), ((), ())), preferred_element_type=F32)


def rows_at(block, count):
    return pl.ds(pl.multiple_of(block * 128, 128), count * 128)


def kernel(
    mat, rest, up, below, linv, out,
    ball, yfwd, rcat, bcat, part, pair, rec_a, rec_b, rec_y, xy, xs, lall, lsplit, acc, acc_in,
    m1, m2, top, mstage, ublk, lstage, sums, sums_in,
    in_sem, r_sem, m_sem, send, recv,
):
    z = lax.axis_index("row_0")
    yh = lax.axis_index("row_1")
    yl = lax.axis_index("col_0")
    x = lax.axis_index("col_1")
    h = lax.axis_index("col_2")
    me_r = z * 2 + yh
    y = yh * 2 + yl

    def dev(dz=0, dyh=0, dyl=0, dx=0, dh=0):
        return ((z + dz) % 4, (yh + dyh) % 2, (yl + dyl) % 2, (x + dx) % 4, (h + dh) % 2)

    def dev_y(dy):
        there = (y + dy) % 4
        return (z, there // 2, there % 2, x, h)

    def copy(src, dst, index, device):
        return pltpu.make_async_remote_copy(
            src_ref=src, dst_ref=dst, send_sem=send.at[index], recv_sem=recv.at[index],
            device_id=device, device_id_type=MESH,
        )

    partner = dev(dh=1)
    zp, zm = dev(dz=1), dev(dz=3)
    xp, xm = dev(dx=1), dev(dx=3)
    yp, ym = dev_y(1), dev_y(3)
    ypair = dev(dyl=1)

    load_below = [pltpu.make_async_copy(below.at[k], ball.at[me_r, k], in_sem.at[k]) for k in range(2)]
    load_l = pltpu.make_async_copy(linv, lstage, in_sem.at[2])
    load_u = pltpu.make_async_copy(up, ublk, in_sem.at[3])
    load_top = pltpu.make_async_copy(mat.at[pl.ds(0, 2)], top, in_sem.at[4])

    def staged(p):
        return (p // 4, (p // 2) % 2, pl.ds(pl.multiple_of((p % 2) * 896, 128), 896))

    def load_r(p):
        return pltpu.make_async_copy(rest.at[p], part.at[staged(p)], r_sem.at[p])

    def load_m(p):
        return pltpu.make_async_copy(mat.at[p], mstage.at[p % 2], m_sem.at[p % 2])

    for load in (*load_below, load_l):
        load.start()
    for p in range(16):
        load_r(p).start()
    load_u.start()
    load_top.start()

    barrier = pltpu.get_barrier_semaphore()
    friends = [dev(dz=dz, dyh=dyh) for dz in range(4) for dyh in range(2) if (dz, dyh) != (0, 0)]
    friends += [dev(dx=dx, dh=dh) for dx in range(4) for dh in range(2) if (dx, dh) != (0, 0)]
    friends += [yp, ym]
    for friend in friends:
        pl.semaphore_signal(barrier, inc=1, device_id=friend, device_id_type=MESH)

    sums[...] = jnp.zeros(sums.shape, F32)

    def take_r(p, carry):
        load_r(p).wait()
        where = pl.ds(pl.multiple_of(((p // 4) * 4 + (p % 2) * 2 + (p // 2) % 2) * 128, 128), 128)
        total = jnp.zeros((8, 128), F32)
        for q in range(7):
            rows = pl.ds(pl.multiple_of((p % 2) * 896 + q * 128, 128), 128)
            value = part[p // 4, (p // 2) % 2, rows]
            total += jnp.sum((value * value).reshape(16, 8, 128), axis=0)
            hi, lo = split(value)
            rcat[where, q * 128:(q + 1) * 128] = hi
            rcat[where, (7 + q) * 128:(8 + q) * 128] = lo
        sums[0, 1] += total
        return carry

    lax.fori_loop(0, 8, take_r, 0)
    for load in load_below:
        load.wait()
    load_l.wait()
    pl.semaphore_wait(barrier, len(friends))

    def below_copy(source, half, step, device):
        ref = ball.at[source, half]
        return copy(ref, ref, S_BELOW + 2 * step + half, device)

    below_copy(me_r, 0, 1, zp).start()
    below_copy(me_r, 1, 2, zm).start()
    copy(ball.at[me_r, 0], yfwd.at[0], S_FWD, yp).start()
    copy(ball.at[me_r, 1], yfwd.at[1], S_FWD + 1, ym).start()

    my_l = lall.at[yl, yh, x, z]
    lanes = pl.ds(pl.multiple_of(h * 128, 128), 128)
    swap_l = copy(lstage.at[1 - h], lall.at[yl, yh, x, z, :, lanes], S_L, partner)
    swap_l.start()
    for core in range(2):
        @pl.when(h == core)
        def _():
            lall[yl, yh, x, z, :, core * 128:(core + 1) * 128] = lstage[core]

    lax.fori_loop(8, 16, take_r, 0)
    load_u.wait()

    mine_l = jnp.logical_or(h == 1, yl == 0)
    beside_l = jnp.logical_or(h == 1, yl == 1)
    swap_l.wait_recv()

    def lz_copies():
        return [copy(my_l, my_l, S_L + j, dev(dz=j)) for j in range(1, 4)]

    def lx_copy(side):
        ref = lall.at[yl, yh, x]
        return copy(ref, ref, S_L + 4 + side, xp if side == 0 else xm)

    def lx_forward(side):
        ref = lall.at[yl, yh, (x + (3 if side == 0 else 1)) % 4, pl.ds(2 * side, 2)]
        return copy(ref, ref, S_L + 6 + side, xp if side == 0 else xm)

    @pl.when(mine_l)
    def _():
        for c in lz_copies():
            c.start()

    below_copy(me_r, 1, 1, zp).start()
    below_copy(me_r, 0, 2, zm).start()

    def ly_copy(side, from_dy, xq, zq):
        there = (y + from_dy) % 4
        ref = lall.at[there % 2, there // 2, xq, zq]
        if side == 2:
            even = (xq + zq) % 2 == 0
            target = (y + jnp.where(even, 1, 3)) % 4
            device = (z, target // 2, target % 2, x, h)
        else:
            device = yp if side == 0 else ym
        return copy(ref, ref, S_LY + 16 * side + xq * 4 + zq, device)

    def needed(yl_from, xq, zq):
        return jnp.logical_or(h != yl_from, xq <= zq)

    def ly_each(dx, yl_from, fn):
        xq = (x + dx) % 4
        for zq in range(4):
            @pl.when(needed(yl_from, xq, zq))
            def _():
                fn(xq, zq)

    def ly_start(dx):
        @pl.when(mine_l)
        def _():
            def fn(xq, zq):
                ly_copy(0, 0, xq, zq).start()
                ly_copy(1, 0, xq, zq).start()

            ly_each(dx, yl, fn)

    def ly_forward(dx):
        @pl.when(beside_l)
        def _():
            def fn(xq, zq):
                ly_copy(0, 3, xq, zq).wait_recv()
                ly_copy(1, 1, xq, zq).wait_recv()
                from_dy = jnp.where((xq + zq) % 2 == 0, 3, 1)
                ly_copy(2, from_dy, xq, zq).start()

            ly_each(dx, 1 - yl, fn)

    def source(step):
        dz = jnp.where(jnp.logical_or(step == 1, step == 5), 3, jnp.where(jnp.logical_or(step == 2, step == 6), 1, 0))
        dz = jnp.where(jnp.logical_or(step == 4, step == 7), 2, dz)
        dy = jnp.where(jnp.logical_or(step == 3, step >= 5), 1, 0)
        return (z + dz) % 4, (yh + dy) % 2

    def source_row(step):
        zs, ys = source(step)
        return zs * 2 + ys

    def pair_copy(s, share):
        where = rows_at(share * 4, 4)
        return copy(part.at[s % 4, 1 - h, where], pair.at[s, where], S_PAIR + 4 * s + share, partner)

    def add_pair(s, share):
        pair_copy(s, share).wait_recv()

        def add(i, carry):
            where = rows_at(share * 4 + i, 1)
            part[s % 4, h, where] += pair[s, where]
            return carry

        lax.fori_loop(0, 4, add, 0)

    def a_copy(s, side):
        far = (x + 2) % 4
        src = part.at[s % 4, h, rows_at(far * 4 + 2 * side, 2)]
        return copy(src, rec_a.at[s, side], S_A + 2 * s + side, xp if side == 0 else xm)

    def b_copy(s, side):
        near = (x + (1 if side == 0 else 3)) % 4
        src = part.at[s % 4, h, rows_at(near * 4, 4)]
        return copy(src, rec_b.at[s, side], S_B + 2 * s + side, xp if side == 0 else xm)

    def y_copy(s):
        return copy(xy.at[s, rows_at((1 - yl) * 2, 2)], rec_y.at[s], S_Y + s, ypair)

    def step_body(t, carry):
        @pl.when(t < 8)
        def _():
            load_m(2 * t).start()
            load_m(2 * t + 1).start()

        @pl.when(t == 1)
        def _():
            below_copy(source_row(1), 0, 1, zp).wait_recv()
            below_copy(source_row(1), 0, 4, zp).start()
            below_copy(source_row(2), 1, 2, zm).wait_recv()
            below_copy(source_row(2), 1, 4, zm).start()

        @pl.when(t == 2)
        def _():
            @pl.when(mine_l)
            def _():
                for c in lz_copies():
                    c.wait_recv()
                lx_copy(0).start()
                lx_copy(1).start()

            ly_start(0)

        @pl.when(t == 3)
        def _():
            r = source_row(3)
            below_copy(r, 0, 3, zp).wait_recv()
            below_copy(r, 1, 3, zp).wait_recv()
            below_copy(r, 0, 5, zp).start()
            below_copy(r, 1, 6, zm).start()
            below_copy(r, 1, 5, zp).start()
            below_copy(r, 0, 6, zm).start()

        @pl.when(t == 4)
        def _():
            @pl.when(mine_l)
            def _():
                lx_copy(0).wait_recv()
                lx_forward(0).start()
                lx_copy(1).wait_recv()
                lx_forward(1).start()

            ly_start(1)
            ly_start(3)
            ly_forward(0)

        @pl.when(t == 5)
        def _():
            below_copy(source_row(5), 0, 5, zp).wait_recv()
            below_copy(source_row(5), 0, 7, zp).start()
            below_copy(source_row(6), 1, 6, zm).wait_recv()
            below_copy(source_row(6), 1, 7, zm).start()

            @pl.when(mine_l)
            def _():
                lx_forward(0).wait_recv()
                lx_forward(1).wait_recv()

            ly_start(2)

        @pl.when(t == 7)
        def _():
            ly_forward(1)
            ly_forward(3)

        @pl.when(t < 8)
        def _():
            r = source_row(t)
            seen = jnp.logical_or(t == 0, t == 3)
            seen0 = jnp.logical_or(seen, jnp.logical_or(t == 1, t == 5))
            seen1 = jnp.logical_or(seen, jnp.logical_or(t == 2, t == 6))

            @pl.when(jnp.logical_not(seen0))
            def _():
                below_copy(r, 0, t, zp).wait_recv()

            @pl.when(jnp.logical_not(seen1))
            def _():
                below_copy(r, 1, t, zp).wait_recv()

            for k in range(2):
                for q in range(7):
                    hi, lo = split(ball[r, k, q])
                    where = slice(k * 128, (k + 1) * 128)
                    bcat[where, q * 128:(q + 1) * 128] = hi
                    bcat[where, (7 + q) * 128:(8 + q) * 128] = hi
                    bcat[where, (14 + q) * 128:(15 + q) * 128] = lo

            def quarter(i, carry):
                share = (x + 2 + i) % 4
                for u in range(2):
                    where = rows_at(share * 4 + 2 * u, 2)
                    value = dot_t(rcat[where, 0:1792], bcat[:, 0:1792]) + dot_t(rcat[where, 0:896], bcat[:, 1792:2688])
                    part[t % 4, 0, where] = value[:, :128]
                    part[t % 4, 1, where] = value[:, 128:]

                @pl.when(jnp.logical_and((yl * 8 + x * 2 + h) % 8 == r, share == 0))
                def _():
                    for k in range(2):
                        part[t % 4, yl, k * 256:k * 256 + 128] -= ublk[k]

                pair_copy(t, share).start()
                return carry

            lax.fori_loop(0, 4, quarter, 0)

            for slot in range(2):
                load_m(2 * t + slot).wait()
                value = mstage[slot]
                sums[0, 0] += jnp.sum((value * value).reshape(128, 8, 128), axis=0)

            add_pair(t, (x + 2) % 4)
            a_copy(t, 0).start()
            a_copy(t, 1).start()

        @pl.when(t == 0)
        def _():
            copy(yfwd.at[0], yfwd.at[0], S_FWD, yp).wait_recv()
            copy(yfwd.at[1], yfwd.at[1], S_FWD + 1, ym).wait_recv()
            back = (y + 3) % 4
            copy(yfwd.at[0], ball.at[z * 2 + back // 2, 0], S_BELOW + 6, yp).start()
            ahead = (y + 1) % 4
            copy(yfwd.at[1], ball.at[z * 2 + ahead // 2, 1], S_BELOW + 7, ym).start()

        @pl.when(jnp.logical_and(t >= 1, t < 9))
        def _():
            s = t - 1
            for side in range(2):
                near = (x + (1 if side == 0 else 3)) % 4
                add_pair(s, near)
                a_copy(s, side).wait_recv()
                where = rows_at(near * 4 + 2 * side, 2)
                part[s % 4, h, where] += rec_a[s, side]
                b_copy(s, side).start()
            add_pair(s, x)

        @pl.when(t >= 2)
        def _():
            s = t - 2
            b_copy(s, 0).wait_recv()
            b_copy(s, 1).wait_recv()

            def add(i, carry):
                where = rows_at(i, 1)
                xy[s, where] = part[s % 4, h, rows_at(x * 4 + i, 1)] + rec_b[s, 0, where] + rec_b[s, 1, where]
                return carry

            lax.fori_loop(0, 4, add, 0)
            y_copy(s).start()
            for share in range(4):
                pair_copy(s, share).wait_send()
            for side in range(2):
                a_copy(s, side).wait_send()
                b_copy(s, side).wait_send()

        return carry

    lax.fori_loop(0, 10, step_body, 0)

    ly_forward(2)

    def take_y(s, carry):
        y_copy(s).wait_recv()
        hi, lo = split(xy[s, rows_at(yl * 2, 2)] + rec_y[s])
        xs[0, source_row(s)] = hi
        xs[1, source_row(s)] = lo
        return carry

    lax.fori_loop(0, 8, take_y, 0)

    def ly_last(fn):
        @pl.when(mine_l)
        def _():
            for dx in range(4):
                ly_each(dx, yl, fn)

    ly_last(lambda xq, zq: ly_copy(2, 2, xq, zq).wait_recv())

    def product(i):
        for r in range(8):
            piece = lall[i // 4, r % 2, i % 4, r // 2]
            hi, lo = split(jnp.where(needed(i // 4, i % 4, r // 2), piece, 0.0))
            lsplit[0, r * 128:(r + 1) * 128] = hi
            lsplit[1, r * 128:(r + 1) * 128] = lo
        left = jnp.concatenate([xs[0, r] for r in range(8)], axis=1)
        rest_of = jnp.concatenate([xs[1, r] for r in range(8)], axis=1)
        acc[i] = dot_n(left, lsplit[0]) + dot_n(rest_of, lsplit[0]) + dot_n(left, lsplit[1])

    def out_copy(i):
        return copy(acc.at[i], acc_in.at[i], S_OUT + i, partner)

    def mirror_row(j, side):
        to_z = (z + j) % 4
        src = acc.at[4 * h + to_z, :, side * 128:(side + 1) * 128]
        other = jnp.where(yh == side, 0, 1)
        return copy(src, m1.at[me_r], S_M1 + 2 * j + other, (to_z, side, yl, x, h))

    def mirror_row_in(j, other):
        from_z, from_y = (z + 4 - j) % 4, (yh + other) % 2
        ref = m1.at[from_z * 2 + from_y]
        return copy(ref, ref, S_M1 + 2 * j + other, zp)

    @pl.when(h == 1)
    def _():
        def early(j, carry):
            i = (z + 1 + j) % 4
            product(i)
            out_copy(i).start()
            return carry

        lax.fori_loop(0, 4, early, 0)

    def late(j0, carry):
        j = (j0 + 1) % 4
        i = (z + j) % 4
        product(4 * h + i)

        @pl.when(h == 0)
        def _():
            out_copy(i).wait_recv()
            acc[i] += acc_in[i]

        value = acc[4 * h + i]
        value = value * value
        sums[0, 1] += jnp.sum((value[:, :128] + value[:, 128:]).reshape(32, 8, 128), axis=0)
        for side in range(2):
            @pl.when(jnp.logical_or(j != 0, yh != side))
            def _():
                mirror_row(j, side).start()

            @pl.when(jnp.logical_and(j == 0, yh == side))
            def _():
                m1[me_r] = acc[4 * h + z, :, side * 128:(side + 1) * 128]

        return carry

    lax.fori_loop(0, 4, late, 0)

    def sum_copy(phase, slot, device):
        return copy(sums.at[phase], sums_in.at[3 * phase + slot], S_SUM + 3 * phase + slot - (2 if phase else 0), device)

    def sum_copies(phase):
        if phase == 0:
            return [sum_copy(0, 0, partner)]
        make = (None, lambda j: dev(dx=j), dev_y, lambda j: dev(dz=j))[phase]
        return [sum_copy(phase, j - 1, make(j)) for j in range(1, 4)]

    for c in sum_copies(0):
        c.start()

    for phase in range(4):
        copies = sum_copies(phase)
        for c in copies:
            c.wait_recv()
        total = sums[phase]
        for slot in range(len(copies)):
            total += sums_in[3 * phase + slot]
        sums[phase + 1] = total
        if phase < 3:
            for c in sum_copies(phase + 1):
                c.start()

    def mirror_col(to_x, to_h):
        index = S_M2 + 2 * ((to_x + 4 - x) % 4) + (to_h + h) % 2
        return copy(m1.at[to_x * 2 + to_h], m2.at[h, x], index, (z, yh, yl, to_x, to_h))

    def mirror_col_in(j):
        from_x, from_h = (x + 4 - j // 2) % 4, (h + j % 2) % 2
        ref = m2.at[from_h, from_x]
        return copy(ref, ref, S_M2 + j, xp)

    def spread(j, carry):
        from_z, from_y = (z + 4 - j // 2) % 4, (yh + j % 2) % 2

        @pl.when(j > 0)
        def _():
            mirror_row_in(j // 2, j % 2).wait_recv()

        here = jnp.logical_and(from_z == x, from_y == h)

        @pl.when(here)
        def _():
            m2[h, x] = m1[x * 2 + h]

        @pl.when(jnp.logical_not(here))
        def _():
            mirror_col(from_z, from_y).start()

        return carry

    lax.fori_loop(0, 8, spread, 0)

    load_top.wait()
    total = sums[4]
    ratio = jnp.sum(total[1], axis=(0, 1), keepdims=True) / jnp.sum(total[0], axis=(0, 1), keepdims=True)
    balance = jnp.sqrt(jnp.sqrt(ratio))
    half = 0.5 * balance
    inverse = -0.5 / balance

    def finish(j, carry):
        @pl.when(j > 0)
        def _():
            mirror_col_in(j).wait_recv()

        k, xf = (h + j % 2) % 2, (x + 4 - j // 2) % 4
        for m in range(2):
            block = m2[k, xf, m * 128:(m + 1) * 128]
            where = pl.ds(2 * xf + m, 128, stride=8)
            out[k, where, :] = half * top[k, where, :] + inverse * block.T
        return carry

    lax.fori_loop(0, 8, finish, 0)

    for step in range(1, 8):
        for side in range(2):
            below_copy(me_r, side, step, zp).wait_send()
    for side in range(2):
        copy(ball.at[me_r, side], yfwd.at[side], S_FWD + side, yp).wait_send()
    swap_l.wait_send()

    @pl.when(mine_l)
    def _():
        for c in lz_copies():
            c.wait_send()
        for side in range(2):
            lx_copy(side).wait_send()
            lx_forward(side).wait_send()

    def ly_sent(xq, zq):
        ly_copy(0, 0, xq, zq).wait_send()
        ly_copy(1, 0, xq, zq).wait_send()

    ly_last(ly_sent)

    @pl.when(beside_l)
    def _():
        for dx in range(4):
            ly_each(dx, 1 - yl, lambda xq, zq: ly_copy(2, 1, xq, zq).wait_send())

    def last_y(s, carry):
        y_copy(s).wait_send()
        return carry

    lax.fori_loop(0, 8, last_y, 0)

    @pl.when(h == 1)
    def _():
        for i in range(4):
            out_copy(i).wait_send()

    def last_mirror(j, carry):
        copy(m1.at[0], m1.at[0], S_M1 + j, zp).wait_send()
        copy(m1.at[0], m1.at[0], S_M2 + j, xp).wait_send()
        return carry

    lax.fori_loop(1, 8, last_mirror, 0)
    for phase in range(4):
        for c in sum_copies(phase):
            c.wait_send()


def per_device(matrix, inverse_rest, upper_block, lower_below, lower_inverse):
    vmem = pltpu.VMEM
    dma = pltpu.SemaphoreType.DMA
    result = pl.pallas_call(
        kernel,
        out_shape=jax.ShapeDtypeStruct((2, 1024, 128), F32),
        in_specs=[pl.BlockSpec(memory_space=ANY)] * 5,
        out_specs=pl.BlockSpec(memory_space=pltpu.VMEM),
        scratch_shapes=[
            vmem((8, 2, 7, 128, 128), F32),
            vmem((2, 7, 128, 128), F32),
            vmem((2048, 1792), BF16),
            vmem((256, 2688), BF16),
            vmem((4, 2, 2048, 128), F32),
            vmem((8, 2048, 128), F32),
            vmem((8, 2, 256, 128), F32),
            vmem((8, 2, 512, 128), F32),
            vmem((8, 256, 128), F32),
            vmem((8, 512, 128), F32),
            vmem((2, 8, 256, 128), BF16),
            vmem((2, 2, 4, 4, 128, 256), F32),
            vmem((2, 1024, 256), BF16),
            vmem((8, 256, 256), F32),
            vmem((4, 256, 256), F32),
            vmem((8, 256, 128), F32),
            vmem((2, 4, 256, 128), F32),
            vmem((2, 1024, 128), F32),
            vmem((2, 1024, 128), F32),
            vmem((2, 128, 128), F32),
            vmem((2, 128, 128), F32),
            vmem((5, 2, 8, 128), F32),
            vmem((12, 2, 8, 128), F32),
            dma((5,)),
            dma((16,)),
            dma((2,)),
            dma((N_SEM,)),
            dma((N_SEM,)),
        ],
        compiler_params=pltpu.CompilerParams(
            collective_id=0, has_side_effects=True, vmem_limit_bytes=67043328
        ),
    )(
        matrix.reshape(16, 1024, 128),
        inverse_rest.transpose(0, 2, 1, 3).reshape(16, 896, 128),
        upper_block.reshape(2, 128, 128),
        lower_below.transpose(0, 2, 1, 3),
        lower_inverse,
    )
    return result.reshape(2, 128, 8, 128)


def solution(mesh):
    split_mesh = Mesh(mesh.devices.reshape(4, 2, 2, 4, 2), ("row_0", "row_1", "col_0", "col_1", "col_2"))
    return jax.shard_map(
        per_device,
        mesh=split_mesh,
        in_specs=(
            P(None, ROW, None, COL),
            P(None, ROW, None, COL),
            P(None, ROW, None, COL),
            P(None, ROW, None, COL),
            P(None, ROW, COL),
        ),
        out_specs=P(None, ROW, None, COL),
        check_vma=False,
    )
```

time: 238 us -> 169 us (0.71)
  Pallas kernels: 235 us -> 167 us
    pallas_call x1, Pallas kernels: 235 us -> 167 us  [per_device(): pl.pallas_call(kernel, out_shape=jax.ShapeDtypeStruct((2, 1024, 128), F32...]
where the time goes in v2:
time: 169 us
  Pallas kernels  167 us (99%)
  local copies, waits for them, and re-layouts  2.26 us (1%)
    pallas_call x1, Pallas kernels, per_device(): pl.pallas_call(kernel, out_shape=jax.ShapeDtypeStruct((2, 1024, 128), F32...  167 us

profile of v2, /device:TPU:1, one launch (start us, length us, event | category | flops | bytes accessed | tf_op | source)
XLA Modules:
  0.0 168.9 jit_solution(13322423913601455357)
XLA Ops:
  0.0 166.6 %shard_map.55 = f32[2,1024,128]{2,1,0:T(8,128)} custom-call(f32[16,1024,128]{2,1,0:T(8,128)} %bitcast.7, f32[16,896,128]{2,1,0:T(8,128)} %bitcast.8, f32[2,128,128]{2,1,0:T(8,128)} %bitcast.11, f32[2,7,128,128]{3,2,1,0:T(8,128)} %bitcast.10, f32[2,128,128]{2,1,0:T(8,128)} %linv.1), custom_call_target="tpu_custom_call" | custom-call | tf_op jit(solution)/shard_map/pallas_call | solution.py:619
  166.6 2.3 %copy.7 = f32[2,128,8,128]{3,2,1,0:T(8,128)} copy(f32[2,128,8,128]{3,2,1,0:T(8,128)} %bitcast.9) | data formatting | bytes 2097152

commit v3 on v2

--- a/solution.py
+++ b/solution.py
@@ -20,12 +20,14 @@
 S_B = 66
 S_Y = 82
 S_L = 90
-S_LY = 98
-S_OUT = 146
-S_M1 = 150
-S_M2 = 158
-S_SUM = 166
-N_SEM = 176
+S_L2 = 94
+S_LY = 106
+S_OUT = 154
+S_M1 = 158
+S_M2 = 166
+S_MF = 174
+S_SUM = 177
+N_SEM = 199
 
 
 def split(value):
@@ -49,7 +51,7 @@
 def kernel(
     mat, rest, up, below, linv, out,
     ball, yfwd, rcat, bcat, part, pair, rec_a, rec_b, rec_y, xy, xs, lall, lsplit, acc, acc_in,
-    m1, m2, top, mstage, ublk, lstage, sums, sums_in,
+    m1, m2, mfwd, top, mstage, ublk, lstage, sums, sums_in,
     in_sem, r_sem, m_sem, send, recv,
 ):
     z = lax.axis_index("row_0")
@@ -101,9 +103,12 @@
     load_top.start()
 
     barrier = pltpu.get_barrier_semaphore()
-    friends = [dev(dz=dz, dyh=dyh) for dz in range(4) for dyh in range(2) if (dz, dyh) != (0, 0)]
-    friends += [dev(dx=dx, dh=dh) for dx in range(4) for dh in range(2) if (dx, dh) != (0, 0)]
-    friends += [yp, ym]
+    def dev_zy(dz, dy):
+        there = (y + dy) % 4
+        return ((z + dz) % 4, there // 2, there % 2, x, h)
+
+    friends = [dev_zy(j // 4, j % 4) for j in range(1, 16)]
+    friends += [dev(dx=j // 2, dh=j % 2) for j in range(1, 8)]
     for friend in friends:
         pl.semaphore_signal(barrier, inc=1, device_id=friend, device_id_type=MESH)
 
@@ -134,7 +139,7 @@
         return copy(ref, ref, S_BELOW + 2 * step + half, device)
 
     below_copy(me_r, 0, 1, zp).start()
-    below_copy(me_r, 1, 2, zm).start()
+    below_copy(me_r, 1, 1, zm).start()
     copy(ball.at[me_r, 0], yfwd.at[0], S_FWD, yp).start()
     copy(ball.at[me_r, 1], yfwd.at[1], S_FWD + 1, ym).start()
 
@@ -154,75 +159,90 @@
     beside_l = jnp.logical_or(h == 1, yl == 1)
     swap_l.wait_recv()
 
-    def lz_copies():
-        return [copy(my_l, my_l, S_L + j, dev(dz=j)) for j in range(1, 4)]
-
-    def lx_copy(side):
-        ref = lall.at[yl, yh, x]
-        return copy(ref, ref, S_L + 4 + side, xp if side == 0 else xm)
-
-    def lx_forward(side):
-        ref = lall.at[yl, yh, (x + (3 if side == 0 else 1)) % 4, pl.ds(2 * side, 2)]
-        return copy(ref, ref, S_L + 6 + side, xp if side == 0 else xm)
-
-    @pl.when(mine_l)
-    def _():
-        for c in lz_copies():
-            c.start()
-
-    below_copy(me_r, 1, 1, zp).start()
-    below_copy(me_r, 0, 2, zm).start()
-
-    def ly_copy(side, from_dy, xq, zq):
-        there = (y + from_dy) % 4
-        ref = lall.at[there % 2, there // 2, xq, zq]
+    def piece_at(i, d):
+        return jnp.where(h == 0, (x + d) % 4, i), jnp.where(h == 0, i, (z + d) % 4)
+
+    def dev_first(d):
+        return (jnp.where(h == 0, (z + d) % 4, z), yh, yl, jnp.where(h == 0, x, (x + d) % 4), h)
+
+    def dev_second(d):
+        return (jnp.where(h == 0, z, (z + d) % 4), yh, yl, jnp.where(h == 0, (x + d) % 4, x), h)
+
+    def needed(yl_from, xq, zq):
+        return jnp.logical_or(h != yl_from, xq <= zq)
+
+    def l1_copy(j):
+        return copy(my_l, my_l, S_L + j, dev_first(j))
+
+    def l1_wait(j):
+        @pl.when(needed(yl, jnp.where(h == 0, x, (x + 4 - j) % 4), jnp.where(h == 0, (z + 4 - j) % 4, z)))
+        def _():
+            l1_copy(j).wait_recv()
+
+    def l2_copy(side, i):
+        xq, zq = piece_at(i, 0)
+        ref = lall.at[yl, yh, xq, zq]
+        return copy(ref, ref, S_L2 + 4 * side + i, dev_second(1 if side == 0 else 3))
+
+    def l2_forward(i):
+        xq, zq = piece_at(i, 3 if i % 2 == 0 else 1)
+        ref = lall.at[yl, yh, xq, zq]
+        return copy(ref, ref, S_L2 + 8 + i, dev_second(1 if i % 2 == 0 else 3))
+
+    def l_each(d, yl_from, fn):
+        for i in range(4):
+            xq, zq = piece_at(i, d)
+
+            def one(i=i, xq=xq, zq=zq):
+                fn(i, xq, zq)
+
+            pl.when(needed(yl_from, xq, zq))(one)
+
+    def ly_copy(side, xq, zq):
         if side == 2:
-            even = (xq + zq) % 2 == 0
-            target = (y + jnp.where(even, 1, 3)) % 4
+            there = (y + jnp.where(yl == 1, 3, 1)) % 4
+            target = (y + jnp.where(yl == 1, 1, 3)) % 4
+            ref = lall.at[there % 2, there // 2, xq, zq]
             device = (z, target // 2, target % 2, x, h)
         else:
+            ref = lall.at[yl, yh, xq, zq]
             device = yp if side == 0 else ym
         return copy(ref, ref, S_LY + 16 * side + xq * 4 + zq, device)
 
-    def needed(yl_from, xq, zq):
-        return jnp.logical_or(h != yl_from, xq <= zq)
-
-    def ly_each(dx, yl_from, fn):
-        xq = (x + dx) % 4
-        for zq in range(4):
-            @pl.when(needed(yl_from, xq, zq))
-            def _():
-                fn(xq, zq)
-
-    def ly_start(dx):
+    def ly_start(d):
         @pl.when(mine_l)
         def _():
-            def fn(xq, zq):
-                ly_copy(0, 0, xq, zq).start()
-                ly_copy(1, 0, xq, zq).start()
-
-            ly_each(dx, yl, fn)
-
-    def ly_forward(dx):
+            def fn(i, xq, zq):
+                ly_copy(0, xq, zq).start()
+                ly_copy(1, xq, zq).start()
+
+            l_each(d, yl, fn)
+
+    def ly_forward(d):
         @pl.when(beside_l)
         def _():
-            def fn(xq, zq):
-                ly_copy(0, 3, xq, zq).wait_recv()
-                ly_copy(1, 1, xq, zq).wait_recv()
-                from_dy = jnp.where((xq + zq) % 2 == 0, 3, 1)
-                ly_copy(2, from_dy, xq, zq).start()
-
-            ly_each(dx, 1 - yl, fn)
-
-    def source(step):
-        dz = jnp.where(jnp.logical_or(step == 1, step == 5), 3, jnp.where(jnp.logical_or(step == 2, step == 6), 1, 0))
+            def fn(i, xq, zq):
+                ly_copy(0, xq, zq).wait_recv()
+                ly_copy(1, xq, zq).wait_recv()
+                ly_copy(2, xq, zq).start()
+
+            l_each(d, 1 - yl, fn)
+
+    @pl.when(jnp.logical_and(mine_l, needed(yl, x, z)))
+    def _():
+        for j in range(1, 4):
+            l1_copy(j).start()
+
+    below_copy(me_r, 1, 2, zp).start()
+    below_copy(me_r, 0, 2, zm).start()
+
+    def source(step, half):
+        late = jnp.logical_or(step == 3, step >= 5)
+        down = jnp.logical_or(step == 1, step == 5)
+        up = jnp.logical_or(step == 2, step == 6)
+        dz = jnp.where(down, 3 - 2 * half, jnp.where(up, 1 + 2 * half, 0))
         dz = jnp.where(jnp.logical_or(step == 4, step == 7), 2, dz)
-        dy = jnp.where(jnp.logical_or(step == 3, step >= 5), 1, 0)
-        return (z + dz) % 4, (yh + dy) % 2
-
-    def source_row(step):
-        zs, ys = source(step)
-        return zs * 2 + ys
+        return ((z + dz) % 4) * 2 + (yh + jnp.where(late, 1, 0)) % 2
 
     def pair_copy(s, share):
         where = rows_at(share * 4, 4)
@@ -257,84 +277,84 @@
             load_m(2 * t).start()
             load_m(2 * t + 1).start()
 
+        @pl.when(jnp.logical_and(t > 0, t < 8))
+        def _():
+            for k in range(2):
+                below_copy(source(t, k), k, t, zp).wait_recv()
+
         @pl.when(t == 1)
         def _():
-            below_copy(source_row(1), 0, 1, zp).wait_recv()
-            below_copy(source_row(1), 0, 4, zp).start()
-            below_copy(source_row(2), 1, 2, zm).wait_recv()
-            below_copy(source_row(2), 1, 4, zm).start()
+            below_copy(source(1, 0), 0, 4, zp).start()
+            below_copy(source(1, 1), 1, 4, zm).start()
 
         @pl.when(t == 2)
         def _():
             @pl.when(mine_l)
             def _():
-                for c in lz_copies():
-                    c.wait_recv()
-                lx_copy(0).start()
-                lx_copy(1).start()
+                for j in range(1, 4):
+                    l1_wait(j)
+
+                def fn(i, xq, zq):
+                    l2_copy(0, i).start()
+                    l2_copy(1, i).start()
+
+                l_each(0, yl, fn)
 
             ly_start(0)
 
         @pl.when(t == 3)
         def _():
-            r = source_row(3)
-            below_copy(r, 0, 3, zp).wait_recv()
-            below_copy(r, 1, 3, zp).wait_recv()
+            r = source(3, 0)
             below_copy(r, 0, 5, zp).start()
-            below_copy(r, 1, 6, zm).start()
-            below_copy(r, 1, 5, zp).start()
+            below_copy(r, 1, 5, zm).start()
+            below_copy(r, 1, 6, zp).start()
             below_copy(r, 0, 6, zm).start()
 
         @pl.when(t == 4)
         def _():
             @pl.when(mine_l)
             def _():
-                lx_copy(0).wait_recv()
-                lx_forward(0).start()
-                lx_copy(1).wait_recv()
-                lx_forward(1).start()
+                def from_down(i, xq, zq):
+                    l2_copy(0, i).wait_recv()
+                    if i % 2 == 0:
+                        l2_forward(i).start()
+
+                def from_up(i, xq, zq):
+                    l2_copy(1, i).wait_recv()
+                    if i % 2 == 1:
+                        l2_forward(i).start()
+
+                l_each(3, yl, from_down)
+                l_each(1, yl, from_up)
 
             ly_start(1)
             ly_start(3)
+
+        @pl.when(t == 5)
+        def _():
+            below_copy(source(5, 0), 0, 7, zp).start()
+            below_copy(source(5, 1), 1, 7, zm).start()
+
             ly_forward(0)
 
-        @pl.when(t == 5)
-        def _():
-            below_copy(source_row(5), 0, 5, zp).wait_recv()
-            below_copy(source_row(5), 0, 7, zp).start()
-            below_copy(source_row(6), 1, 6, zm).wait_recv()
-            below_copy(source_row(6), 1, 7, zm).start()
-
+        @pl.when(t == 6)
+        def _():
             @pl.when(mine_l)
             def _():
-                lx_forward(0).wait_recv()
-                lx_forward(1).wait_recv()
+                l_each(2, yl, lambda i, xq, zq: l2_forward(i).wait_recv())
 
             ly_start(2)
 
-        @pl.when(t == 7)
+        @pl.when(t == 8)
         def _():
             ly_forward(1)
             ly_forward(3)
 
         @pl.when(t < 8)
         def _():
-            r = source_row(t)
-            seen = jnp.logical_or(t == 0, t == 3)
-            seen0 = jnp.logical_or(seen, jnp.logical_or(t == 1, t == 5))
-            seen1 = jnp.logical_or(seen, jnp.logical_or(t == 2, t == 6))
-
-            @pl.when(jnp.logical_not(seen0))
-            def _():
-                below_copy(r, 0, t, zp).wait_recv()
-
-            @pl.when(jnp.logical_not(seen1))
-            def _():
-                below_copy(r, 1, t, zp).wait_recv()
-
             for k in range(2):
                 for q in range(7):
-                    hi, lo = split(ball[r, k, q])
+                    hi, lo = split(ball[source(t, k), k, q])
                     where = slice(k * 128, (k + 1) * 128)
                     bcat[where, q * 128:(q + 1) * 128] = hi
                     bcat[where, (7 + q) * 128:(8 + q) * 128] = hi
@@ -348,7 +368,7 @@
                     part[t % 4, 0, where] = value[:, :128]
                     part[t % 4, 1, where] = value[:, 128:]
 
-                @pl.when(jnp.logical_and((yl * 8 + x * 2 + h) % 8 == r, share == 0))
+                @pl.when(jnp.logical_and(x * 2 + h == source(t, yl), share == 0))
                 def _():
                     for k in range(2):
                         part[t % 4, yl, k * 256:k * 256 + 128] -= ublk[k]
@@ -416,19 +436,19 @@
     def take_y(s, carry):
         y_copy(s).wait_recv()
         hi, lo = split(xy[s, rows_at(yl * 2, 2)] + rec_y[s])
-        xs[0, source_row(s)] = hi
-        xs[1, source_row(s)] = lo
+        xs[0, source(s, h)] = hi
+        xs[1, source(s, h)] = lo
         return carry
 
     lax.fori_loop(0, 8, take_y, 0)
 
-    def ly_last(fn):
-        @pl.when(mine_l)
-        def _():
-            for dx in range(4):
-                ly_each(dx, yl, fn)
-
-    ly_last(lambda xq, zq: ly_copy(2, 2, xq, zq).wait_recv())
+    def ly_last(yl_from, fn):
+        for d in range(4):
+            l_each(d, yl_from, fn)
+
+    @pl.when(mine_l)
+    def _():
+        ly_last(yl, lambda i, xq, zq: ly_copy(2, xq, zq).wait_recv())
 
     def product(i):
         for r in range(8):
@@ -443,11 +463,25 @@
     def out_copy(i):
         return copy(acc.at[i], acc_in.at[i], S_OUT + i, partner)
 
-    def mirror_row(j, side):
+    def mirror_row(j, side, other):
         to_z = (z + j) % 4
         src = acc.at[4 * h + to_z, :, side * 128:(side + 1) * 128]
-        other = jnp.where(yh == side, 0, 1)
+        if other and j == 0:
+            return copy(src, mfwd.at[0], S_MF, ym)
+        if other and j == 3:
+            return copy(src, mfwd.at[1], S_MF + 1, ym)
+        if other and j == 2:
+            return copy(src, mfwd.at[2], S_MF + 2, zm)
         return copy(src, m1.at[me_r], S_M1 + 2 * j + other, (to_z, side, yl, x, h))
+
+    ahead = ((y + 1) % 4) // 2
+
+    def mirror_row_on(slot):
+        if slot == 0:
+            return copy(mfwd.at[0], m1.at[z * 2 + ahead], S_M1 + 1, ym)
+        if slot == 1:
+            return copy(mfwd.at[1], m1.at[z * 2 + ahead], S_M1 + 7, (zm[0], *ym[1:]))
+        return copy(mfwd.at[2], m1.at[((z + 1) % 4) * 2 + yh], S_M1 + 5, dev(dz=3, dyh=1))
 
     def mirror_row_in(j, other):
         from_z, from_y = (z + 4 - j) % 4, (yh + other) % 2
@@ -457,7 +491,7 @@
     @pl.when(h == 1)
     def _():
         def early(j, carry):
-            i = (z + 1 + j) % 4
+            i = (z + 2 + j) % 4
             product(i)
             out_copy(i).start()
             return carry
@@ -465,7 +499,7 @@
         lax.fori_loop(0, 4, early, 0)
 
     def late(j0, carry):
-        j = (j0 + 1) % 4
+        j = (j0 + 2) % 4
         i = (z + j) % 4
         product(4 * h + i)
 
@@ -478,41 +512,51 @@
         value = value * value
         sums[0, 1] += jnp.sum((value[:, :128] + value[:, 128:]).reshape(32, 8, 128), axis=0)
         for side in range(2):
-            @pl.when(jnp.logical_or(j != 0, yh != side))
-            def _():
-                mirror_row(j, side).start()
-
-            @pl.when(jnp.logical_and(j == 0, yh == side))
-            def _():
-                m1[me_r] = acc[4 * h + z, :, side * 128:(side + 1) * 128]
+            for step in range(4):
+                for other in range(2):
+                    @pl.when(jnp.logical_and(j == step, (yh + other) % 2 == side))
+                    def _():
+                        if step == 0 and other == 0:
+                            m1[me_r] = acc[4 * h + z, :, side * 128:(side + 1) * 128]
+                        else:
+                            mirror_row(step, side, other).start()
 
         return carry
 
     lax.fori_loop(0, 4, late, 0)
-
-    def sum_copy(phase, slot, device):
-        return copy(sums.at[phase], sums_in.at[3 * phase + slot], S_SUM + 3 * phase + slot - (2 if phase else 0), device)
 
     def sum_copies(phase):
         if phase == 0:
-            return [sum_copy(0, 0, partner)]
-        make = (None, lambda j: dev(dx=j), dev_y, lambda j: dev(dz=j))[phase]
-        return [sum_copy(phase, j - 1, make(j)) for j in range(1, 4)]
-
-    for c in sum_copies(0):
-        c.start()
-
-    for phase in range(4):
+            devices = [dev(dx=j // 2, dh=j % 2) for j in range(1, 8)]
+        else:
+            devices = [dev_zy(j // 4, j % 4) for j in range(1, 16)]
+        return [
+            copy(sums.at[phase], sums_in.at[7 * phase + j], S_SUM + 7 * phase + j, device)
+            for j, device in enumerate(devices)
+        ]
+
+    def take_sum(phase):
         copies = sum_copies(phase)
         for c in copies:
             c.wait_recv()
         total = sums[phase]
-        for slot in range(len(copies)):
-            total += sums_in[3 * phase + slot]
-        sums[phase + 1] = total
-        if phase < 3:
-            for c in sum_copies(phase + 1):
-                c.start()
+        for j in range(len(copies)):
+            total += sums_in[7 * phase + j]
+        return total
+
+    for c in sum_copies(0):
+        c.start()
+
+    def send_on(slot):
+        copy(mfwd.at[slot], mfwd.at[slot], S_MF + slot, zp).wait_recv()
+        mirror_row_on(slot).start()
+
+    send_on(2)
+    sums[1] = take_sum(0)
+    for c in sum_copies(1):
+        c.start()
+    send_on(1)
+    send_on(0)
 
     def mirror_col(to_x, to_h):
         index = S_M2 + 2 * ((to_x + 4 - x) % 4) + (to_h + h) % 2
@@ -523,13 +567,10 @@
         ref = m2.at[from_h, from_x]
         return copy(ref, ref, S_M2 + j, xp)
 
-    def spread(j, carry):
+    for j in (0, 2, 6, 4, 3, 5, 7, 1):
         from_z, from_y = (z + 4 - j // 2) % 4, (yh + j % 2) % 2
-
-        @pl.when(j > 0)
-        def _():
+        if j > 0:
             mirror_row_in(j // 2, j % 2).wait_recv()
-
         here = jnp.logical_and(from_z == x, from_y == h)
 
         @pl.when(here)
@@ -540,12 +581,8 @@
         def _():
             mirror_col(from_z, from_y).start()
 
-        return carry
-
-    lax.fori_loop(0, 8, spread, 0)
-
     load_top.wait()
-    total = sums[4]
+    total = take_sum(1)
     ratio = jnp.sum(total[1], axis=(0, 1), keepdims=True) / jnp.sum(total[0], axis=(0, 1), keepdims=True)
     balance = jnp.sqrt(jnp.sqrt(ratio))
     half = 0.5 * balance
@@ -574,22 +611,28 @@
 
     @pl.when(mine_l)
     def _():
-        for c in lz_copies():
-            c.wait_send()
-        for side in range(2):
-            lx_copy(side).wait_send()
-            lx_forward(side).wait_send()
-
-    def ly_sent(xq, zq):
-        ly_copy(0, 0, xq, zq).wait_send()
-        ly_copy(1, 0, xq, zq).wait_send()
-
-    ly_last(ly_sent)
+        @pl.when(needed(yl, x, z))
+        def _():
+            for j in range(1, 4):
+                l1_copy(j).wait_send()
+
+        def l2_sent(i, xq, zq):
+            l2_copy(0, i).wait_send()
+            l2_copy(1, i).wait_send()
+
+        l_each(0, yl, l2_sent)
+        l_each(3, yl, lambda i, xq, zq: l2_forward(i).wait_send() if i % 2 == 0 else None)
+        l_each(1, yl, lambda i, xq, zq: l2_forward(i).wait_send() if i % 2 == 1 else None)
+
+        def ly_sent(i, xq, zq):
+            ly_copy(0, xq, zq).wait_send()
+            ly_copy(1, xq, zq).wait_send()
+
+        ly_last(yl, ly_sent)
 
     @pl.when(beside_l)
     def _():
-        for dx in range(4):
-            ly_each(dx, 1 - yl, lambda xq, zq: ly_copy(2, 1, xq, zq).wait_send())
+        ly_last(1 - yl, lambda i, xq, zq: ly_copy(2, xq, zq).wait_send())
 
     def last_y(s, carry):
         y_copy(s).wait_send()
@@ -608,7 +651,9 @@
         return carry
 
     lax.fori_loop(1, 8, last_mirror, 0)
-    for phase in range(4):
+    for slot in range(3):
+        copy(mfwd.at[slot], mfwd.at[slot], S_MF + slot, zp).wait_send()
+    for phase in range(2):
         for c in sum_copies(phase):
             c.wait_send()
 
@@ -639,12 +684,13 @@
             vmem((4, 256, 256), F32),
             vmem((8, 256, 128), F32),
             vmem((2, 4, 256, 128), F32),
+            vmem((3, 256, 128), F32),
             vmem((2, 1024, 128), F32),
             vmem((2, 1024, 128), F32),
             vmem((2, 128, 128), F32),
             vmem((2, 128, 128), F32),
-            vmem((5, 2, 8, 128), F32),
-            vmem((12, 2, 8, 128), F32),
+            vmem((2, 2, 8, 128), F32),
+            vmem((22, 2, 8, 128), F32),
             dma((5,)),
             dma((16,)),
             dma((2,)),

time: 169 us -> 155 us (0.917); the launches traced: 169 us -> 153 us
  Pallas kernels: 167 us -> 150 us
    pallas_call x1, Pallas kernels: 167 us -> 150 us  [per_device(): pl.pallas_call(kernel, out_shape=jax.ShapeDtypeStruct((2, 1024, 128), F32...]
where the time goes in v3:
time: 155 us; the launch traced here: 153 us
  Pallas kernels  150 us (97%)
  local copies, waits for them, and re-layouts  2.26 us (1%)
    pallas_call x1, Pallas kernels, per_device(): pl.pallas_call(kernel, out_shape=jax.ShapeDtypeStruct((2, 1024, 128), F32...  150 us

profile of v3, /device:TPU:1, one launch (start us, length us, event | category | flops | bytes accessed | tf_op | source)
XLA Modules:
  0.0 152.8 jit_solution(2911385315311023405)
XLA Ops:
  0.0 150.5 %shard_map.55 = f32[2,1024,128]{2,1,0:T(8,128)} custom-call(f32[16,1024,128]{2,1,0:T(8,128)} %bitcast.7, f32[16,896,128]{2,1,0:T(8,128)} %bitcast.8, f32[2,128,128]{2,1,0:T(8,128)} %bitcast.11, f32[2,7,128,128]{3,2,1,0:T(8,128)} %bitcast.10, f32[2,128,128]{2,1,0:T(8,128)} %linv.1), custom_call_target="tpu_custom_call" | custom-call | tf_op jit(solution)/shard_map/pallas_call | solution.py:664
  150.5 2.3 %copy.7 = f32[2,128,8,128]{3,2,1,0:T(8,128)} copy(f32[2,128,8,128]{3,2,1,0:T(8,128)} %bitcast.9) | data formatting | bytes 2097152

commit v4 on v3

--- a/solution.py
+++ b/solution.py
@@ -26,8 +26,8 @@
 S_M1 = 158
 S_M2 = 166
 S_MF = 174
-S_SUM = 177
-N_SEM = 199
+S_SUM = 178
+N_SEM = 200
 
 
 def split(value):
@@ -209,6 +209,10 @@
             device = yp if side == 0 else ym
         return copy(ref, ref, S_LY + 16 * side + xq * 4 + zq, device)
 
+    def ly_wait(side, xq, zq):
+        ref = lall.at[yl, yh, xq, zq]
+        copy(ref, ref, S_LY + 16 * side + xq * 4 + zq, yp).wait_recv()
+
     def ly_start(d):
         @pl.when(mine_l)
         def _():
@@ -222,8 +226,7 @@
         @pl.when(beside_l)
         def _():
             def fn(i, xq, zq):
-                ly_copy(0, xq, zq).wait_recv()
-                ly_copy(1, xq, zq).wait_recv()
+                ly_wait(jnp.where(yl == 1, 0, 1), xq, zq)
                 ly_copy(2, xq, zq).start()
 
             l_each(d, 1 - yl, fn)
@@ -277,16 +280,6 @@
             load_m(2 * t).start()
             load_m(2 * t + 1).start()
 
-        @pl.when(jnp.logical_and(t > 0, t < 8))
-        def _():
-            for k in range(2):
-                below_copy(source(t, k), k, t, zp).wait_recv()
-
-        @pl.when(t == 1)
-        def _():
-            below_copy(source(1, 0), 0, 4, zp).start()
-            below_copy(source(1, 1), 1, 4, zm).start()
-
         @pl.when(t == 2)
         def _():
             @pl.when(mine_l)
@@ -301,14 +294,6 @@
                 l_each(0, yl, fn)
 
             ly_start(0)
-
-        @pl.when(t == 3)
-        def _():
-            r = source(3, 0)
-            below_copy(r, 0, 5, zp).start()
-            below_copy(r, 1, 5, zm).start()
-            below_copy(r, 1, 6, zp).start()
-            below_copy(r, 0, 6, zm).start()
 
         @pl.when(t == 4)
         def _():
@@ -327,14 +312,13 @@
                 l_each(3, yl, from_down)
                 l_each(1, yl, from_up)
 
+            below_copy(source(3, 1), 1, 6, zp).start()
+            below_copy(source(3, 0), 0, 6, zm).start()
             ly_start(1)
             ly_start(3)
 
         @pl.when(t == 5)
         def _():
-            below_copy(source(5, 0), 0, 7, zp).start()
-            below_copy(source(5, 1), 1, 7, zm).start()
-
             ly_forward(0)
 
         @pl.when(t == 6)
@@ -344,11 +328,36 @@
                 l_each(2, yl, lambda i, xq, zq: l2_forward(i).wait_recv())
 
             ly_start(2)
+            ly_forward(1)
+
+        @pl.when(t == 7)
+        def _():
+            ly_forward(3)
 
         @pl.when(t == 8)
         def _():
-            ly_forward(1)
-            ly_forward(3)
+            ly_forward(2)
+
+        @pl.when(jnp.logical_and(t > 0, t < 8))
+        def _():
+            for k in range(2):
+                below_copy(source(t, k), k, t, zp).wait_recv()
+
+        @pl.when(t == 1)
+        def _():
+            below_copy(source(1, 0), 0, 4, zp).start()
+            below_copy(source(1, 1), 1, 4, zm).start()
+
+        @pl.when(t == 3)
+        def _():
+            r = source(3, 0)
+            below_copy(r, 0, 5, zp).start()
+            below_copy(r, 1, 5, zm).start()
+
+        @pl.when(t == 5)
+        def _():
+            below_copy(source(5, 0), 0, 7, zp).start()
+            below_copy(source(5, 1), 1, 7, zm).start()
 
         @pl.when(t < 8)
         def _():
@@ -431,34 +440,49 @@
 
     lax.fori_loop(0, 10, step_body, 0)
 
-    ly_forward(2)
-
     def take_y(s, carry):
         y_copy(s).wait_recv()
         hi, lo = split(xy[s, rows_at(yl * 2, 2)] + rec_y[s])
-        xs[0, source(s, h)] = hi
-        xs[1, source(s, h)] = lo
+        xs[0, s] = hi
+        xs[1, s] = lo
         return carry
-
-    lax.fori_loop(0, 8, take_y, 0)
 
     def ly_last(yl_from, fn):
         for d in range(4):
             l_each(d, yl_from, fn)
 
+    def product(i, first, last):
+        for s in range(first, last):
+            r = source(s, h)
+            piece = lall[i // 4, r % 2, i % 4, r // 2]
+            hi, lo = split(jnp.where(needed(i // 4, i % 4, r // 2), piece, 0.0))
+            lsplit[0, s * 128:(s + 1) * 128] = hi
+            lsplit[1, s * 128:(s + 1) * 128] = lo
+        rows = slice(first * 128, last * 128)
+        left = jnp.concatenate([xs[0, s] for s in range(first, last)], axis=1)
+        rest_of = jnp.concatenate([xs[1, s] for s in range(first, last)], axis=1)
+        value = dot_n(left, lsplit[0, rows]) + dot_n(rest_of, lsplit[0, rows]) + dot_n(left, lsplit[1, rows])
+        if first == 0:
+            acc[i] = value
+        else:
+            acc[i] += value
+
+    def first_part(i, carry):
+        product(i, 0, 6)
+        return carry
+
+    lax.fori_loop(0, 6, take_y, 0)
+
     @pl.when(mine_l)
     def _():
-        ly_last(yl, lambda i, xq, zq: ly_copy(2, xq, zq).wait_recv())
-
-    def product(i):
-        for r in range(8):
-            piece = lall[i // 4, r % 2, i % 4, r // 2]
-            hi, lo = split(jnp.where(needed(i // 4, i % 4, r // 2), piece, 0.0))
-            lsplit[0, r * 128:(r + 1) * 128] = hi
-            lsplit[1, r * 128:(r + 1) * 128] = lo
-        left = jnp.concatenate([xs[0, r] for r in range(8)], axis=1)
-        rest_of = jnp.concatenate([xs[1, r] for r in range(8)], axis=1)
-        acc[i] = dot_n(left, lsplit[0]) + dot_n(rest_of, lsplit[0]) + dot_n(left, lsplit[1])
+        ly_last(yl, lambda i, xq, zq: ly_wait(2, xq, zq))
+
+    @pl.when(beside_l)
+    def _():
+        ly_last(1 - yl, lambda i, xq, zq: ly_wait(jnp.where(yl == 1, 1, 0), xq, zq))
+
+    lax.fori_loop(0, 4 + 4 * h, first_part, 0)
+    lax.fori_loop(6, 8, take_y, 0)
 
     def out_copy(i):
         return copy(acc.at[i], acc_in.at[i], S_OUT + i, partner)
@@ -492,7 +516,7 @@
     def _():
         def early(j, carry):
             i = (z + 2 + j) % 4
-            product(i)
+            product(i, 6, 8)
             out_copy(i).start()
             return carry
 
@@ -501,7 +525,7 @@
     def late(j0, carry):
         j = (j0 + 2) % 4
         i = (z + j) % 4
-        product(4 * h + i)
+        product(4 * h + i, 6, 8)
 
         @pl.when(h == 0)
         def _():
@@ -547,39 +571,53 @@
     for c in sum_copies(0):
         c.start()
 
+    def mirror_col(to_x, to_h):
+        index = S_M2 + 2 * ((to_x + 4 - x) % 4) + (to_h + h) % 2
+        return copy(m1.at[to_x * 2 + to_h], m2.at[h, x], index, (z, yh, yl, to_x, to_h))
+
+    def mirror_col_in(j):
+        from_x, from_h = (x + 4 - j // 2) % 4, (h + j % 2) % 2
+        ref = m2.at[from_h, from_x]
+        return copy(ref, ref, S_M2 + j, xp)
+
     def send_on(slot):
         copy(mfwd.at[slot], mfwd.at[slot], S_MF + slot, zp).wait_recv()
         mirror_row_on(slot).start()
 
+    def spread(j):
+        from_z, from_y = (z + 4 - j // 2) % 4, (yh + j % 2) % 2
+        if j > 0:
+            mirror_row_in(j // 2, j % 2).wait_recv()
+        here = jnp.logical_and(from_z == x, from_y == h)
+
+        @pl.when(here)
+        def _():
+            m2[h, x] = m1[x * 2 + h]
+
+        around = jnp.logical_and(from_z == (x + 2) % 4, j % 2 == 0)
+
+        @pl.when(around)
+        def _():
+            copy(m1.at[from_z * 2 + from_y], mfwd.at[3], S_MF + 3, xm).start()
+
+        @pl.when(jnp.logical_not(jnp.logical_or(here, around)))
+        def _():
+            mirror_col(from_z, from_y).start()
+
+    spread(0)
     send_on(2)
     sums[1] = take_sum(0)
     for c in sum_copies(1):
         c.start()
+    spread(6)
     send_on(1)
     send_on(0)
-
-    def mirror_col(to_x, to_h):
-        index = S_M2 + 2 * ((to_x + 4 - x) % 4) + (to_h + h) % 2
-        return copy(m1.at[to_x * 2 + to_h], m2.at[h, x], index, (z, yh, yl, to_x, to_h))
-
-    def mirror_col_in(j):
-        from_x, from_h = (x + 4 - j // 2) % 4, (h + j % 2) % 2
-        ref = m2.at[from_h, from_x]
-        return copy(ref, ref, S_M2 + j, xp)
-
-    for j in (0, 2, 6, 4, 3, 5, 7, 1):
-        from_z, from_y = (z + 4 - j // 2) % 4, (yh + j % 2) % 2
-        if j > 0:
-            mirror_row_in(j // 2, j % 2).wait_recv()
-        here = jnp.logical_and(from_z == x, from_y == h)
-
-        @pl.when(here)
-        def _():
-            m2[h, x] = m1[x * 2 + h]
-
-        @pl.when(jnp.logical_not(here))
-        def _():
-            mirror_col(from_z, from_y).start()
+    spread(4)
+    spread(2)
+    copy(mfwd.at[3], mfwd.at[3], S_MF + 3, xm).wait_recv()
+    copy(mfwd.at[3], m2.at[h, (x + 1) % 4], S_M2 + 4 + jnp.where(yh == h, 0, 1), (z, yh, yl, (x + 3) % 4, yh)).start()
+    for j in (3, 5, 7, 1):
+        spread(j)
 
     load_top.wait()
     total = take_sum(1)
@@ -651,7 +689,7 @@
         return carry
 
     lax.fori_loop(1, 8, last_mirror, 0)
-    for slot in range(3):
+    for slot in range(4):
         copy(mfwd.at[slot], mfwd.at[slot], S_MF + slot, zp).wait_send()
     for phase in range(2):
         for c in sum_copies(phase):
@@ -684,7 +722,7 @@
             vmem((4, 256, 256), F32),
             vmem((8, 256, 128), F32),
             vmem((2, 4, 256, 128), F32),
-            vmem((3, 256, 128), F32),
+            vmem((4, 256, 128), F32),
             vmem((2, 1024, 128), F32),
             vmem((2, 1024, 128), F32),
             vmem((2, 128, 128), F32),

time: 155 us -> 143 us (0.923); the launches traced: 153 us -> 143 us
  Pallas kernels: 150 us -> 141 us
    pallas_call x1, Pallas kernels: 150 us -> 141 us  [per_device(): pl.pallas_call(kernel, out_shape=jax.ShapeDtypeStruct((2, 1024, 128), F32...]
where the time goes in v4:
time: 143 us
  Pallas kernels  141 us (99%)
  local copies, waits for them, and re-layouts  2.26 us (2%)
    pallas_call x1, Pallas kernels, per_device(): pl.pallas_call(kernel, out_shape=jax.ShapeDtypeStruct((2, 1024, 128), F32...  141 us

profile of v4, /device:TPU:1, one launch (start us, length us, event | category | flops | bytes accessed | tf_op | source)
XLA Modules:
  0.0 143.1 jit_solution(6607479453469440174)
XLA Ops:
  0.0 140.8 %shard_map.55 = f32[2,1024,128]{2,1,0:T(8,128)} custom-call(f32[16,1024,128]{2,1,0:T(8,128)} %bitcast.7, f32[16,896,128]{2,1,0:T(8,128)} %bitcast.8, f32[2,128,128]{2,1,0:T(8,128)} %bitcast.11, f32[2,7,128,128]{3,2,1,0:T(8,128)} %bitcast.10, f32[2,128,128]{2,1,0:T(8,128)} %linv.1), custom_call_target="tpu_custom_call" | custom-call | tf_op jit(solution)/shard_map/pallas_call | solution.py:702
  140.8 2.3 %copy.7 = f32[2,128,8,128]{3,2,1,0:T(8,128)} copy(f32[2,128,8,128]{3,2,1,0:T(8,128)} %bitcast.9) | data formatting | bytes 2097152

commit v5 on v4

--- a/solution.py
+++ b/solution.py
@@ -295,8 +295,14 @@
 
             ly_start(0)
 
+        def second_halves():
+            below_copy(source(3, 1), 1, 6, zp).start()
+            below_copy(source(3, 0), 0, 6, zm).start()
+
         @pl.when(t == 4)
         def _():
+            pl.when(h == 0)(second_halves)
+
             @pl.when(mine_l)
             def _():
                 def from_down(i, xq, zq):
@@ -312,8 +318,7 @@
                 l_each(3, yl, from_down)
                 l_each(1, yl, from_up)
 
-            below_copy(source(3, 1), 1, 6, zp).start()
-            below_copy(source(3, 0), 0, 6, zm).start()
+            pl.when(h == 1)(second_halves)
             ly_start(1)
             ly_start(3)
 
@@ -532,9 +537,6 @@
             out_copy(i).wait_recv()
             acc[i] += acc_in[i]
 
-        value = acc[4 * h + i]
-        value = value * value
-        sums[0, 1] += jnp.sum((value[:, :128] + value[:, 128:]).reshape(32, 8, 128), axis=0)
         for side in range(2):
             for step in range(4):
                 for other in range(2):
@@ -545,6 +547,9 @@
                         else:
                             mirror_row(step, side, other).start()
 
+        value = acc[4 * h + i]
+        value = value * value
+        sums[0, 1] += jnp.sum((value[:, :128] + value[:, 128:]).reshape(32, 8, 128), axis=0)
         return carry
 
     lax.fori_loop(0, 4, late, 0)
@@ -701,7 +706,7 @@
     dma = pltpu.SemaphoreType.DMA
     result = pl.pallas_call(
         kernel,
-        out_shape=jax.ShapeDtypeStruct((2, 1024, 128), F32),
+        out_shape=pltpu.VMEM((2, 1024, 128), F32),
         in_specs=[pl.BlockSpec(memory_space=ANY)] * 5,
         out_specs=pl.BlockSpec(memory_space=pltpu.VMEM),
         scratch_shapes=[
@@ -736,7 +741,7 @@
             dma((N_SEM,)),
         ],
         compiler_params=pltpu.CompilerParams(
-            collective_id=0, has_side_effects=True, vmem_limit_bytes=67043328
+            collective_id=0, has_side_effects=True, vmem_limit_bytes=64500000
         ),
     )(
         matrix.reshape(16, 1024, 128),

time: 143 us -> 141 us (0.986)
  no operation moved by 1% of the time
where the time goes in v5:
time: 141 us
  Pallas kernels  140 us (99%)
    pallas_call x1, Pallas kernels, per_device(): pl.pallas_call(kernel, out_shape=pltpu.VMEM((2, 1024, 128), F32), in_spec...  140 us

profile of v5, /device:TPU:1, one launch (start us, length us, event | category | flops | bytes accessed | tf_op | source)
XLA Modules:
  0.0 140.7 jit_solution(10497397715014083589)
XLA Ops:
  0.0 139.7 %shard_map.55 = f32[2,1024,128]{2,1,0:T(8,128)S(1)} custom-call(f32[16,1024,128]{2,1,0:T(8,128)} %bitcast.8, f32[16,896,128]{2,1,0:T(8,128)} %bitcast.9, f32[2,128,128]{2,1,0:T(8,128)} %bitcast.11, f32[2,7,128,128]{3,2,1,0:T(8,128)} %bitcast.10, f32[2,128,128]{2,1,0:T(8,128)} %linv.1), custom_call_target="tpu_custom_call" | custom-call | tf_op jit(solution)/shard_map/pallas_call | solution.py:707
  139.7 1.0 copy.7

commit v6 on v5

--- a/solution.py
+++ b/solution.py
@@ -392,14 +392,14 @@
 
             lax.fori_loop(0, 4, quarter, 0)
 
+            add_pair(t, (x + 2) % 4)
+            a_copy(t, 0).start()
+            a_copy(t, 1).start()
+
             for slot in range(2):
                 load_m(2 * t + slot).wait()
                 value = mstage[slot]
                 sums[0, 0] += jnp.sum((value * value).reshape(128, 8, 128), axis=0)
-
-            add_pair(t, (x + 2) % 4)
-            a_copy(t, 0).start()
-            a_copy(t, 1).start()
 
         @pl.when(t == 0)
         def _():
@@ -631,7 +631,9 @@
     half = 0.5 * balance
     inverse = -0.5 / balance
 
-    def finish(j, carry):
+    def finish(j0, carry):
+        j = jnp.where(j0 < 4, j0, jnp.where(j0 < 6, j0 + 2, j0 - 2))
+
         @pl.when(j > 0)
         def _():
             mirror_col_in(j).wait_recv()

time: 141 us -> 142 us (level)
  no operation moved by 1% of the time
where the time goes in v6:
time: 142 us; the launch traced here: 141 us
  Pallas kernels  140 us (99%)
    pallas_call x1, Pallas kernels, per_device(): pl.pallas_call(kernel, out_shape=pltpu.VMEM((2, 1024, 128), F32), in_spec...  140 us

profile of v6, /device:TPU:1, one launch (start us, length us, event | category | flops | bytes accessed | tf_op | source)
XLA Modules:
  0.0 141.5 jit_solution(12864147502689360100)
XLA Ops:
  0.0 140.5 %shard_map.55 = f32[2,1024,128]{2,1,0:T(8,128)S(1)} custom-call(f32[16,1024,128]{2,1,0:T(8,128)} %bitcast.8, f32[16,896,128]{2,1,0:T(8,128)} %bitcast.9, f32[2,128,128]{2,1,0:T(8,128)} %bitcast.11, f32[2,7,128,128]{3,2,1,0:T(8,128)} %bitcast.10, f32[2,128,128]{2,1,0:T(8,128)} %linv.1), custom_call_target="tpu_custom_call" | custom-call | tf_op jit(solution)/shard_map/pallas_call | solution.py:709
  140.5 1.0 copy.7
